TPU v7x, 32 devices: a whole 2x2x4 slice. The times are simulated.
32 devices in a mesh: row: 8 (over z, x), col: 4 (over y, core).
Axes of the slice: x: 2, y: 2, z: 4, core: 2. Of those that a mesh axis runs over, the one named last changes fastest.
Arguments:
- values: bfloat16 [8, 4, 2, 128, 128], P('row', 'col'), may hold values from -6 to 6
- occupancy: int32 [8, 4, 2], replicated, may hold values from 0 to 8, as said below
Outputs:
- square: bfloat16 [8, 4, 2, 128, 128], P('row', 'col')
- updated: float32 [8, 4, 2, 128, 128], P('row', 'col')
Inputs may be any that keep to these rules, and one draw needn't show every extreme that they name: `occupancy`: within each tile the slots that are not 2 * 4 name distinct positions; a slot holding 2 * 4 is empty. Every tile has one or more stored blocks; in every draw some tile has all 2 slots stored and some tile has an empty slot.
All inputs are finite; a program needn't handle non-finite values.
Results may differ from a plain program's by a relative error of at most 0.0018.
Values may be sent and summed in bfloat16 or wider, within the bound.
No kernel may reach another device: no remote copies, remote signals or barrier semaphores. Data moves between devices by JAX's collectives and lax.ppermute only.
A program may use at most 64 MiB of HBM per device.

v0:
```python
import functools
import math

import jax
import jax.numpy as jnp
from jax import lax
from jax.experimental import pallas as pl
from jax.experimental.pallas import tpu as pltpu
from jax.sharding import PartitionSpec as P


RB = 2


def routes(row_count, col_count):
    inner = 2 if row_count % 2 == 0 else 1
    far = [inner * z for z in range(2, row_count // inner)]
    order = [(f"r{k}", "row", None, k) for k in reversed(far)]
    near = [k for k in (1, 3, 2) if k < row_count and k not in far]
    order += [(f"r{k}", "row", None, k) for k in near]
    half = [k for k in range(1, col_count) if k == 1 or k % 2 == 0]
    order += [(f"c{k}", "col", None, k) for k in half]
    if inner == 2:
        order += [(f"r{k + 1}", "row", f"r{k}", 1) for k in reversed(far)]
    order += [(f"c{k + 1}", "col", f"c{k}", 1) for k in half if k > 1]
    return order


def gather(own, row_count, col_count):
    sizes = {"row": row_count, "col": col_count}
    held = {}
    for name, axis, source, offset in routes(row_count, col_count):
        held[name] = lax.ppermute(
            own if source is None else held[source],
            axis,
            [(i, i ^ offset) for i in range(sizes[axis])],
        )
    rights = [held[f"r{k}"] for k in range(1, row_count)]
    lefts = [held[f"c{k}"] for k in range(1, col_count)]
    return rights, lefts


def regather(square, col_count):
    held = {}
    for name, axis, source, offset in routes(1, col_count):
        held[name] = lax.ppermute(
            square if source is None else held[source],
            axis,
            [(i, i ^ offset) for i in range(col_count)],
        )
    return [held[f"c{k}"] for k in range(1, col_count)]


def split(number, divisor):
    if divisor & (divisor - 1) == 0:
        return number >> (divisor.bit_length() - 1), number & (divisor - 1)
    return lax.div(number, divisor), lax.rem(number, divisor)


def stage_kernel(values, own):
    own[...] = values[...]


def plan_kernel(sizes, occ, plan):
    row_count, col_count, slots, tile_rows, tile_cols, room = sizes
    row, col = lax.axis_index("row"), lax.axis_index("col")
    positions = tile_rows * tile_cols
    mine = [occ[col, s, row] for s in range(slots)]
    lines = [split(q, tile_cols) for q in mine]
    lines = [(line * tile_cols, jnp.where(q < positions, c, -1)) for q, (line, c) in zip(mine, lines)]
    ends = [jnp.int32(s * room + 1) for s in range(slots)]
    for offset in range(row_count):
        tile = row ^ offset
        for u in range(slots):
            q = occ[col, u, tile]
            line, column = split(q, tile_cols)
            panel, depth = split(tile * tile_rows + jnp.minimum(line, tile_rows - 1), tile_cols)
            column = jnp.where(q < positions, column, -2)
            base = (panel ^ col) * slots
            held = [occ[panel, v, row] for v in range(slots)]
            for s in range(slots):
                wanted = jnp.where(lines[s][1] == column, lines[s][0] + depth, -1)
                place = base
                hit = held[0] == wanted
                for v in range(1, slots):
                    also = held[v] == wanted
                    place = jnp.where(also, base + v, place)
                    hit = hit | also
                plan[ends[s]] = place
                plan[ends[s] + 1] = jnp.int32(offset * slots + u)
                ends[s] = ends[s] + jnp.where(hit, 2, 0)
    for s in range(slots):
        plan[s * room] = (ends[s] - (s * room + 1)) >> 1
        plan[(s + 1) * room - 1] = (mine[s] < positions).astype(jnp.int32)
        plan[ends[s]] = jnp.int32(col_count * slots)
        plan[ends[s] + 1] = jnp.int32(0)


def pair_sums(plan, room, left, right, slots):
    counts = [plan[s * room] for s in range(slots)]
    most = functools.reduce(jnp.maximum, counts)
    zero_block = left.shape[0] - 1

    def step(turn, totals):
        result = []
        for s in range(slots):
            lefts, rights = [], []
            for half in range(2):
                at = 2 * turn + half
                live = at < counts[s]
                at = s * room + 1 + 2 * jnp.minimum(at, counts[s])
                lefts.append(left[jnp.where(live, plan[at], zero_block)])
                rights.append(right[plan[at + 1]])
            product = jnp.dot(
                jnp.concatenate(lefts, axis=1),
                jnp.concatenate(rights, axis=0),
                preferred_element_type=jnp.float32,
            )
            result.append(totals[s] + product)
        return tuple(result)

    block = right.shape[-1]
    zeros = tuple(jnp.zeros((block, block), jnp.float32) for _ in range(slots))
    return lax.fori_loop(0, (most + 1) // 2, step, zeros)


def stack(target, tiles, slots):
    for at, tile in enumerate(tiles):
        target[at * slots : (at + 1) * slots] = tile[...]


def square_kernel(sizes, factor, *refs):
    row_count, col_count, slots, _, _, room = sizes
    plan_in = refs[0]
    rights = refs[1 : 1 + row_count]
    lefts = refs[1 + row_count : row_count + col_count]
    out, left, right, plan, sem = refs[row_count + col_count :]
    copy = pltpu.make_async_copy(plan_in, plan, sem)
    copy.start()
    stack(right, rights, slots)
    stack(left, (rights[0],) + lefts, slots)
    left[col_count * slots] = jnp.zeros(left.shape[1:], left.dtype)
    copy.wait()
    sums = pair_sums(plan, room, left, right, slots)
    for s in range(slots):
        out[s] = (factor * sums[s]).astype(out.dtype)


def cube_kernel(sizes, factor, *refs):
    row_count, col_count, slots, _, _, room = sizes
    plan_in = refs[0]
    rights = refs[1 : 1 + row_count]
    lefts = refs[1 + row_count : 1 + row_count + col_count]
    square, updated, left, right, result, plan, sem, square_sem, out_sem = refs[1 + row_count + col_count :]
    square_copy = pltpu.make_async_copy(lefts[0], square, square_sem)
    square_copy.start()
    copy = pltpu.make_async_copy(plan_in, plan, sem)
    copy.start()
    stack(right, rights, slots)
    stack(left, lefts, slots)
    left[col_count * slots] = jnp.zeros(left.shape[1:], left.dtype)
    copy.wait()
    sums = pair_sums(plan, room, left, right, slots)
    copies = []
    for s in range(slots):
        stored = plan[(s + 1) * room - 1].astype(jnp.float32)
        own = rights[0][s].astype(jnp.float32) * stored
        result[s] = 1.5 * own - (0.5 * factor) * sums[s]
        copies.append(pltpu.make_async_copy(result.at[s], updated.at[s], out_sem.at[s]))
        copies[-1].start()
    for done in copies:
        done.wait()
    square_copy.wait()


def per_device(values, occupancy):
    row_count = lax.axis_size("row")
    col_count = lax.axis_size("col")
    slots = values.shape[2]
    block = values.shape[-1]
    tile_rows = RB
    tile_cols = RB * row_count // col_count
    factor = 5.0 / math.sqrt(tile_rows * block * row_count)
    room = 2 * (row_count * slots + 1) + 2
    sizes = (row_count, col_count, slots, tile_rows, tile_cols, room)
    values = values.reshape(slots, block, block)
    vmem = pl.BlockSpec(memory_space=pltpu.VMEM)
    smem = pl.BlockSpec(memory_space=pltpu.SMEM)
    anywhere = pl.BlockSpec(memory_space=pl.ANY)
    limit = pltpu.CompilerParams(vmem_limit_bytes=24 * 1024 * 1024)
    tile = jax.ShapeDtypeStruct((slots, block, block), jnp.bfloat16)
    dma = pltpu.SemaphoreType.DMA
    scratch = [
        pltpu.VMEM((col_count * slots + 1, block, block), jnp.bfloat16),
        pltpu.VMEM((row_count * slots, block, block), jnp.bfloat16),
    ]
    own = pl.pallas_call(
        stage_kernel,
        out_shape=tile,
        in_specs=[vmem],
        out_specs=vmem,
        compiler_params=limit,
        name="stage",
    )(values)
    rights, lefts = gather(own, row_count, col_count)
    plan = pl.pallas_call(
        functools.partial(plan_kernel, sizes),
        out_shape=jax.ShapeDtypeStruct((slots * room,), jnp.int32),
        in_specs=[smem],
        out_specs=smem,
        compiler_params=limit,
        name="plan",
    )(occupancy.transpose(1, 2, 0))
    square = pl.pallas_call(
        functools.partial(square_kernel, sizes, factor),
        out_shape=tile,
        in_specs=[anywhere] + [vmem] * (row_count + col_count - 1),
        out_specs=vmem,
        scratch_shapes=scratch + [pltpu.SMEM((slots * room,), jnp.int32), dma],
        compiler_params=limit,
        name="square",
    )(plan, own, *rights, *lefts)
    others = regather(square, col_count)
    square_out, updated = pl.pallas_call(
        functools.partial(cube_kernel, sizes, factor),
        out_shape=(tile, jax.ShapeDtypeStruct((slots, block, block), jnp.float32)),
        in_specs=[anywhere] + [vmem] * (row_count + col_count),
        out_specs=(anywhere, anywhere),
        scratch_shapes=scratch
        + [
            pltpu.VMEM((slots, block, block), jnp.float32),
            pltpu.SMEM((slots * room,), jnp.int32),
            dma,
            dma,
            dma((slots,)),
        ],
        compiler_params=limit,
        name="cube",
    )(plan, own, *rights, square, *others)
    shape_out = (1, 1, slots, block, block)
    return (square_out.reshape(shape_out), updated.reshape(shape_out))


def solution(mesh):
    spec = P("row", "col", None, None, None)

    return jax.shard_map(
        per_device,
        mesh=mesh,
        in_specs=(spec, P()),
        out_specs=(spec, spec),
        check_vma=False,
    )
```

profile of v0, /device:TPU:0, one launch (start us, length us, event | category | flops | bytes accessed | tf_op | source)
XLA Modules:
  0.0 27.9 jit_solution(15719484465996454637)
XLA Ops:
  0.6 0.0 copy-start
  0.6 0.8 %copy-done = bf16[1,1,2,128,128]{4,3,2,1,0:T(8,128)(2,1)S(1)} copy-done((bf16[1,1,2,128,128]{4,3,2,1,0:T(8,128)(2,1)S(1)}, bf16[1,1,2,128,128]{4,3,2,1,0:T(8,128)(2,1)}, u32[]{:S(2)}) %copy-start) | copy-done | bytes 65560
  1.5 3.1 %collective-permute-start.8 = (bf16[2,128,128]{2,1,0:T(8,128)(2,1)S(1)}, bf16[2,128,128]{2,1,0:T(8,128)(2,1)S(1)}, u32[]{:S(2)}, u32[]{:S(2)}) collective-permute-start(bf16[2,128,128]{2,1,0:T(8,128)(2,1)S(1)} %stage.1.refs_1_), channel_id=1, source_target_pairs={{0,2},{1,3},{2,0},{3,1},{4,6},{5,7},{6,4},{7,5},{8,10},{9,11},{10,... | collective-permute-start | bytes 196616 | tf_op jit(solution)/shard_map/ppermute | solution.py:33
  4.5 0.0 collective-permute-start.7
  4.5 3.6 %collective-permute-start.5 = (bf16[2,128,128]{2,1,0:T(8,128)(2,1)S(1)}, bf16[2,128,128]{2,1,0:T(8,128)(2,1)S(1)}, u32[]{:S(2)}, u32[]{:S(2)}) collective-permute-start(bf16[2,128,128]{2,1,0:T(8,128)(2,1)S(1)} %stage.1.refs_1_), channel_id=1, source_target_pairs={{0,24},{4,28},{8,16},{12,20},{16,8},{20,12},{24,0},{28,4},{1,25},{... | collective-permute-start | bytes 196616 | tf_op jit(solution)/shard_map/ppermute | solution.py:33
  8.1 0.0 collective-permute-start.3
  8.1 1.7 %collective-permute-start.2 = (bf16[2,128,128]{2,1,0:T(8,128)(2,1)S(1)}, bf16[2,128,128]{2,1,0:T(8,128)(2,1)S(1)}, u32[]{:S(2)}, u32[]{:S(2)}) collective-permute-start(bf16[2,128,128]{2,1,0:T(8,128)(2,1)S(1)} %stage.1.refs_1_), channel_id=1, source_target_pairs={{0,12},{4,8},{8,4},{12,0},{16,28},{20,24},{24,20},{28,16},{1,13},{... | collective-permute-start | bytes 196616 | tf_op jit(solution)/shard_map/ppermute | solution.py:33
  9.9 0.0 collective-permute-done.8.refs_10_
  9.9 1.2 %collective-permute-start.1 = (bf16[2,128,128]{2,1,0:T(8,128)(2,1)S(1)}, bf16[2,128,128]{2,1,0:T(8,128)(2,1)S(1)}, u32[]{:S(2)}, u32[]{:S(2)}) collective-permute-start(bf16[2,128,128]{2,1,0:T(8,128)(2,1)S(1)} %stage.1.refs_1_), channel_id=1, source_target_pairs={{0,8},{4,12},{8,0},{12,4},{16,24},{20,28},{24,16},{28,20},{1,9},{5... | collective-permute-start | bytes 196616 | tf_op jit(solution)/shard_map/ppermute | solution.py:33
  11.1 0.0 collective-permute-done.7.refs_9_
  11.1 0.5 %collective-permute-start = (bf16[2,128,128]{2,1,0:T(8,128)(2,1)S(1)}, bf16[2,128,128]{2,1,0:T(8,128)(2,1)S(1)}, u32[]{:S(2)}, u32[]{:S(2)}) collective-permute-start(bf16[2,128,128]{2,1,0:T(8,128)(2,1)S(1)} %stage.1.refs_1_), channel_id=1, source_target_pairs={{0,4},{4,0},{8,12},{12,8},{16,20},{20,16},{24,28},{28,24},{1,5},{5... | collective-permute-start | bytes 196616 | tf_op jit(solution)/shard_map/ppermute | solution.py:33
  11.6 0.0 collective-permute-done.5.refs_7_
  11.6 0.0 collective-permute-start.9
  11.6 2.7 %collective-permute-done.3.refs_5_ = bf16[2,128,128]{2,1,0:T(8,128)(2,1)S(1)} collective-permute-done((bf16[2,128,128]{2,1,0:T(8,128)(2,1)S(1)}, bf16[2,128,128]{2,1,0:T(8,128)(2,1)S(1)}, u32[]{:S(2)}, u32[]{:S(2)}) %collective-permute-start.3) | collective-permute-done | bytes 65568 | tf_op jit(solution)/shard_map/ppermute | solution.py:33
  14.4 1.5 %collective-permute-start.6 = (bf16[2,128,128]{2,1,0:T(8,128)(2,1)S(1)}, bf16[2,128,128]{2,1,0:T(8,128)(2,1)S(1)}, u32[]{:S(2)}, u32[]{:S(2)}) collective-permute-start(bf16[2,128,128]{2,1,0:T(8,128)(2,1)S(1)} %collective-permute-done.5.refs_7_), channel_id=1, source_target_pairs={{0,4},{4,0},{8,12},{12,8},{16,20},{20,16},{24,28},{28,24},{1,5},{5... | collective-permute-start | bytes 196616 | tf_op jit(solution)/shard_map/ppermute | solution.py:33
  15.9 0.0 collective-permute-done.2.refs_4_
  15.9 0.9 %collective-permute-start.4 = (bf16[2,128,128]{2,1,0:T(8,128)(2,1)S(1)}, bf16[2,128,128]{2,1,0:T(8,128)(2,1)S(1)}, u32[]{:S(2)}, u32[]{:S(2)}) collective-permute-start(bf16[2,128,128]{2,1,0:T(8,128)(2,1)S(1)} %collective-permute-done.3.refs_5_), channel_id=1, source_target_pairs={{0,4},{4,0},{8,12},{12,8},{16,20},{20,16},{24,28},{28,24},{1,5},{5... | collective-permute-start | bytes 196616 | tf_op jit(solution)/shard_map/ppermute | solution.py:33
  16.8 0.0 copy-done.1
  16.8 1.5 %plan.1.refs_0_ = s32[72]{0:T(128)S(1)} custom-call(s32[4,2,8]{2,1,0:T(2,128)S(1)} %bitcast.5), custom_call_target="tpu_custom_call" | custom-call | tf_op jit(solution)/shard_map/plan/pallas_call | solution.py:206
  18.3 0.0 collective-permute-done.1.refs_3_
  18.3 0.0 collective-permute-done.refs_2_
  18.3 0.0 collective-permute-done.9.refs_11_
  18.3 0.8 %collective-permute-done.6.refs_8_ = bf16[2,128,128]{2,1,0:T(8,128)(2,1)S(1)} collective-permute-done((bf16[2,128,128]{2,1,0:T(8,128)(2,1)S(1)}, bf16[2,128,128]{2,1,0:T(8,128)(2,1)S(1)}, u32[]{:S(2)}, u32[]{:S(2)}) %collective-permute-start.6) | collective-permute-done | bytes 65568 | tf_op jit(solution)/shard_map/ppermute | solution.py:33
  19.1 1.0 %collective-permute-done.4.refs_6_ = bf16[2,128,128]{2,1,0:T(8,128)(2,1)S(1)} collective-permute-done((bf16[2,128,128]{2,1,0:T(8,128)(2,1)S(1)}, bf16[2,128,128]{2,1,0:T(8,128)(2,1)S(1)}, u32[]{:S(2)}, u32[]{:S(2)}) %collective-permute-start.4) | collective-permute-done | bytes 65568 | tf_op jit(solution)/shard_map/ppermute | solution.py:33
  20.1 0.8 %square.1.refs_9_ = bf16[2,128,128]{2,1,0:T(8,128)(2,1)S(1)} custom-call(s32[72]{0:T(128)S(1)} %plan.1.refs_0_, bf16[2,128,128]{2,1,0:T(8,128)(2,1)S(1)} %stage.1.refs_1_, bf16[2,128,128]{2,1,0:T(8,128)(2,1)S(1)} %collective-permute-done.refs_2_, bf16[2,128,128]{2,1,0:T(8,128)(2,1)S(1)} %collective-permute-done.1.refs_3_, ...), custom_call_target="tpu_custom_call" | custom-call | tf_op jit(solution)/shard_map/square/pallas_call | solution.py:214
  20.9 0.4 %collective-permute-start.11 = (bf16[2,128,128]{2,1,0:T(8,128)(2,1)S(1)}, bf16[2,128,128]{2,1,0:T(8,128)(2,1)S(1)}, u32[]{:S(2)}, u32[]{:S(2)}) collective-permute-start(bf16[2,128,128]{2,1,0:T(8,128)(2,1)S(1)} %square.1.refs_9_), channel_id=1, source_target_pairs={{0,2},{1,3},{2,0},{3,1},{4,6},{5,7},{6,4},{7,5},{8,10},{9,11},{10,... | collective-permute-start | bytes 196616 | tf_op jit(solution)/shard_map/ppermute | solution.py:46
  21.3 0.0 collective-permute-start.10
  21.3 3.9 %collective-permute-done.11.refs_11_ = bf16[2,128,128]{2,1,0:T(8,128)(2,1)S(1)} collective-permute-done((bf16[2,128,128]{2,1,0:T(8,128)(2,1)S(1)}, bf16[2,128,128]{2,1,0:T(8,128)(2,1)S(1)}, u32[]{:S(2)}, u32[]{:S(2)}) %collective-permute-start.11) | collective-permute-done | bytes 65568 | tf_op jit(solution)/shard_map/ppermute | solution.py:46
  25.2 0.0 collective-permute-start.12
  25.2 0.0 collective-permute-done.10.refs_10_
  25.2 1.2 %collective-permute-done.12.refs_12_ = bf16[2,128,128]{2,1,0:T(8,128)(2,1)S(1)} collective-permute-done((bf16[2,128,128]{2,1,0:T(8,128)(2,1)S(1)}, bf16[2,128,128]{2,1,0:T(8,128)(2,1)S(1)}, u32[]{:S(2)}, u32[]{:S(2)}) %collective-permute-start.12) | collective-permute-done | bytes 65568 | tf_op jit(solution)/shard_map/ppermute | solution.py:46
  26.5 1.4 %cube.1 = (bf16[2,128,128]{2,1,0:T(8,128)(2,1)}, f32[2,128,128]{2,1,0:T(8,128)}) custom-call(s32[72]{0:T(128)S(1)} %plan.1.refs_0_, bf16[2,128,128]{2,1,0:T(8,128)(2,1)S(1)} %stage.1.refs_1_, bf16[2,128,128]{2,1,0:T(8,128)(2,1)S(1)} %collective-permute-done.refs_2_, bf16[2,128,128]{2,1,0:T(8,128)(2,1)S(1)} %collective-permute-done.1.refs_3_, ...), custom_call_target="tpu_custom_call" | custom-call | tf_op jit(solution)/shard_map/cube/pallas_call | solution.py:224
  (2 shorter events, 0.0 us)
Async XLA Ops:
  0.6 0.8 %copy-start = (bf16[1,1,2,128,128]{4,3,2,1,0:T(8,128)(2,1)S(1)}, bf16[1,1,2,128,128]{4,3,2,1,0:T(8,128)(2,1)}, u32[]{:S(2)}) copy-start(bf16[1,1,2,128,128]{4,3,2,1,0:T(8,128)(2,1)} %param.2) | copy-start | bytes 196612
  1.5 15.3 %copy-start.1 = (s32[8,4,2]{0,2,1:T(2,128)S(1)}, s32[8,4,2]{0,2,1:T(2,128)}, u32[]{:S(2)}) copy-start(s32[8,4,2]{0,2,1:T(2,128)} %param.3) | copy-start | bytes 772
  1.5 8.4 %collective-permute-start.8 = (bf16[2,128,128]{2,1,0:T(8,128)(2,1)S(1)}, bf16[2,128,128]{2,1,0:T(8,128)(2,1)S(1)}, u32[]{:S(2)}, u32[]{:S(2)}) collective-permute-start(bf16[2,128,128]{2,1,0:T(8,128)(2,1)S(1)} %stage.1.refs_1_), channel_id=1, source_target_pairs={{0,2},{1,3},{2,0},{3,1},{4,6},{5,7},{6,4},{7,5},{8,10},{9,11},{10,... | collective-permute-start | bytes 196616 | tf_op jit(solution)/shard_map/ppermute | solution.py:33
  4.5 6.6 %collective-permute-start.7 = (bf16[2,128,128]{2,1,0:T(8,128)(2,1)S(1)}, bf16[2,128,128]{2,1,0:T(8,128)(2,1)S(1)}, u32[]{:S(2)}, u32[]{:S(2)}) collective-permute-start(bf16[2,128,128]{2,1,0:T(8,128)(2,1)S(1)} %stage.1.refs_1_), channel_id=1, source_target_pairs={{0,1},{1,0},{2,3},{3,2},{4,5},{5,4},{6,7},{7,6},{8,9},{9,8},{10,11... | collective-permute-start | bytes 196616 | tf_op jit(solution)/shard_map/ppermute | solution.py:33
  4.5 7.1 %collective-permute-start.5 = (bf16[2,128,128]{2,1,0:T(8,128)(2,1)S(1)}, bf16[2,128,128]{2,1,0:T(8,128)(2,1)S(1)}, u32[]{:S(2)}, u32[]{:S(2)}) collective-permute-start(bf16[2,128,128]{2,1,0:T(8,128)(2,1)S(1)} %stage.1.refs_1_), channel_id=1, source_target_pairs={{0,24},{4,28},{8,16},{12,20},{16,8},{20,12},{24,0},{28,4},{1,25},{... | collective-permute-start | bytes 196616 | tf_op jit(solution)/shard_map/ppermute | solution.py:33
  8.1 6.2 %collective-permute-start.3 = (bf16[2,128,128]{2,1,0:T(8,128)(2,1)S(1)}, bf16[2,128,128]{2,1,0:T(8,128)(2,1)S(1)}, u32[]{:S(2)}, u32[]{:S(2)}) collective-permute-start(bf16[2,128,128]{2,1,0:T(8,128)(2,1)S(1)} %stage.1.refs_1_), channel_id=1, source_target_pairs={{0,16},{4,20},{8,24},{12,28},{16,0},{20,4},{24,8},{28,12},{1,17},{... | collective-permute-start | bytes 196616 | tf_op jit(solution)/shard_map/ppermute | solution.py:33
  8.1 7.7 %collective-permute-start.2 = (bf16[2,128,128]{2,1,0:T(8,128)(2,1)S(1)}, bf16[2,128,128]{2,1,0:T(8,128)(2,1)S(1)}, u32[]{:S(2)}, u32[]{:S(2)}) collective-permute-start(bf16[2,128,128]{2,1,0:T(8,128)(2,1)S(1)} %stage.1.refs_1_), channel_id=1, source_target_pairs={{0,12},{4,8},{8,4},{12,0},{16,28},{20,24},{24,20},{28,16},{1,13},{... | collective-permute-start | bytes 196616 | tf_op jit(solution)/shard_map/ppermute | solution.py:33
  9.9 8.4 %collective-permute-start.1 = (bf16[2,128,128]{2,1,0:T(8,128)(2,1)S(1)}, bf16[2,128,128]{2,1,0:T(8,128)(2,1)S(1)}, u32[]{:S(2)}, u32[]{:S(2)}) collective-permute-start(bf16[2,128,128]{2,1,0:T(8,128)(2,1)S(1)} %stage.1.refs_1_), channel_id=1, source_target_pairs={{0,8},{4,12},{8,0},{12,4},{16,24},{20,28},{24,16},{28,20},{1,9},{5... | collective-permute-start | bytes 196616 | tf_op jit(solution)/shard_map/ppermute | solution.py:33
  11.1 7.2 %collective-permute-start = (bf16[2,128,128]{2,1,0:T(8,128)(2,1)S(1)}, bf16[2,128,128]{2,1,0:T(8,128)(2,1)S(1)}, u32[]{:S(2)}, u32[]{:S(2)}) collective-permute-start(bf16[2,128,128]{2,1,0:T(8,128)(2,1)S(1)} %stage.1.refs_1_), channel_id=1, source_target_pairs={{0,4},{4,0},{8,12},{12,8},{16,20},{20,16},{24,28},{28,24},{1,5},{5... | collective-permute-start | bytes 196616 | tf_op jit(solution)/shard_map/ppermute | solution.py:33
  11.6 6.7 %collective-permute-start.9 = (bf16[2,128,128]{2,1,0:T(8,128)(2,1)S(1)}, bf16[2,128,128]{2,1,0:T(8,128)(2,1)S(1)}, u32[]{:S(2)}, u32[]{:S(2)}) collective-permute-start(bf16[2,128,128]{2,1,0:T(8,128)(2,1)S(1)} %collective-permute-done.8.refs_10_), channel_id=1, source_target_pairs={{0,1},{1,0},{2,3},{3,2},{4,5},{5,4},{6,7},{7,6},{8,9},{9,8},{10,11... | collective-permute-start | bytes 196616 | tf_op jit(solution)/shard_map/ppermute | solution.py:33
  14.4 4.8 %collective-permute-start.6 = (bf16[2,128,128]{2,1,0:T(8,128)(2,1)S(1)}, bf16[2,128,128]{2,1,0:T(8,128)(2,1)S(1)}, u32[]{:S(2)}, u32[]{:S(2)}) collective-permute-start(bf16[2,128,128]{2,1,0:T(8,128)(2,1)S(1)} %collective-permute-done.5.refs_7_), channel_id=1, source_target_pairs={{0,4},{4,0},{8,12},{12,8},{16,20},{20,16},{24,28},{28,24},{1,5},{5... | collective-permute-start | bytes 196616 | tf_op jit(solution)/shard_map/ppermute | solution.py:33
  15.9 4.3 %collective-permute-start.4 = (bf16[2,128,128]{2,1,0:T(8,128)(2,1)S(1)}, bf16[2,128,128]{2,1,0:T(8,128)(2,1)S(1)}, u32[]{:S(2)}, u32[]{:S(2)}) collective-permute-start(bf16[2,128,128]{2,1,0:T(8,128)(2,1)S(1)} %collective-permute-done.3.refs_5_), channel_id=1, source_target_pairs={{0,4},{4,0},{8,12},{12,8},{16,20},{20,16},{24,28},{28,24},{1,5},{5... | collective-permute-start | bytes 196616 | tf_op jit(solution)/shard_map/ppermute | solution.py:33
  20.9 4.3 %collective-permute-start.11 = (bf16[2,128,128]{2,1,0:T(8,128)(2,1)S(1)}, bf16[2,128,128]{2,1,0:T(8,128)(2,1)S(1)}, u32[]{:S(2)}, u32[]{:S(2)}) collective-permute-start(bf16[2,128,128]{2,1,0:T(8,128)(2,1)S(1)} %square.1.refs_9_), channel_id=1, source_target_pairs={{0,2},{1,3},{2,0},{3,1},{4,6},{5,7},{6,4},{7,5},{8,10},{9,11},{10,... | collective-permute-start | bytes 196616 | tf_op jit(solution)/shard_map/ppermute | solution.py:46
  21.3 4.0 %collective-permute-start.10 = (bf16[2,128,128]{2,1,0:T(8,128)(2,1)S(1)}, bf16[2,128,128]{2,1,0:T(8,128)(2,1)S(1)}, u32[]{:S(2)}, u32[]{:S(2)}) collective-permute-start(bf16[2,128,128]{2,1,0:T(8,128)(2,1)S(1)} %square.1.refs_9_), channel_id=1, source_target_pairs={{0,1},{1,0},{2,3},{3,2},{4,5},{5,4},{6,7},{7,6},{8,9},{9,8},{10,11... | collective-permute-start | bytes 196616 | tf_op jit(solution)/shard_map/ppermute | solution.py:46
  25.2 1.3 %collective-permute-start.12 = (bf16[2,128,128]{2,1,0:T(8,128)(2,1)S(1)}, bf16[2,128,128]{2,1,0:T(8,128)(2,1)S(1)}, u32[]{:S(2)}, u32[]{:S(2)}) collective-permute-start(bf16[2,128,128]{2,1,0:T(8,128)(2,1)S(1)} %collective-permute-done.11.refs_11_), channel_id=1, source_target_pairs={{0,1},{1,0},{2,3},{3,2},{4,5},{5,4},{6,7},{7,6},{8,9},{9,8},{10,11... | collective-permute-start | bytes 196616 | tf_op jit(solution)/shard_map/ppermute | solution.py:46
where the time goes:
time: 28.1 us; the launch traced here: 27.9 us
  starting transfers between devices  13 us (46%)
  waiting for transfers between devices  9.73 us (35%)
  Pallas kernels  3.71 us (13%)
  local copies, waits for them, and re-layouts  0.84 us (3%)
  between operations  0.69 us (2%)
    ppermute x10, starting transfers between devices, gather(): lax.ppermute(own if source is None else held[source], axis, [(i, i ^ offs...  12.6 us
    ppermute x3, waiting for transfers between devices, regather(): lax.ppermute(square if source is None else held[source], axis, [(i, i ^ o...  5.2 us
    ppermute x10, waiting for transfers between devices, gather(): lax.ppermute(own if source is None else held[source], axis, [(i, i ^ offs...  4.54 us
    pallas_call x1, Pallas kernels, per_device(): pl.pallas_call(functools.partial(plan_kernel, sizes), out_shape=jax.Shape...  1.5 us
    pallas_call x1, Pallas kernels, per_device(): pl.pallas_call(functools.partial(cube_kernel, sizes, factor), out_shape=(...  1.45 us
    unnamed x4, local copies, waits for them, and re-layouts  0.84 us
    pallas_call x1, Pallas kernels, per_device(): pl.pallas_call(functools.partial(square_kernel, sizes, factor), out_shape...  0.76 us
  transfers between devices with their start and end apart: 13, of which 5 were waited for; matrix products, arithmetic and copies ran while one was open for 0% of the time, Pallas kernels for 5%

commit v1 on v0

v1 whole, which is shorter than its diff:
```python
import functools
import math

import jax
import jax.numpy as jnp
from jax import lax
from jax.experimental import pallas as pl
from jax.experimental.pallas import tpu as pltpu
from jax.sharding import PartitionSpec as P


RB = 2
PARAMS = pltpu.CompilerParams(vmem_limit_bytes=24 * 1024 * 1024)
VMEM = pl.BlockSpec(memory_space=pltpu.VMEM)
SMEM = pl.BlockSpec(memory_space=pltpu.SMEM)
ANY = pl.BlockSpec(memory_space=pl.ANY)


def send(array, axis, offset):
    size = lax.axis_size(axis)
    return lax.ppermute(array, axis, [(i, i ^ offset) for i in range(size)])


def join_kernel(*refs):
    at = 0
    for ref in refs[:-1]:
        refs[-1][at : at + ref.shape[0]] = ref[...]
        at += ref.shape[0]


def join(*arrays):
    shape = (sum(a.shape[0] for a in arrays),) + arrays[0].shape[1:]
    return pl.pallas_call(
        join_kernel,
        out_shape=jax.ShapeDtypeStruct(shape, arrays[0].dtype),
        in_specs=[VMEM] * len(arrays),
        out_specs=VMEM,
        compiler_params=PARAMS,
        name="join",
    )(*arrays)


def far_rows(row_count):
    return list(range(row_count - 2, 2, -2))


def column_order(row_count):
    far = far_rows(row_count)
    early = [0] + far + [2, 1]
    late = [3] + [k + 1 for k in far]
    return early, late


def gather(own, row_count, col_count):
    far = far_rows(row_count)
    rows = {k: send(own, "row", k) for k in far + [2]}
    near = send(own, "col", 1)
    rows[1] = send(own, "row", 1)
    pair = join(own, near)
    lefts = [near] + [send(pair, "col", k) for k in range(2, col_count, 2)]
    late = [send(join(rows[2], rows[far[0]]), "row", 1)]
    late += [send(rows[k], "row", 1) for k in far[1:]]
    return [rows[k] for k in far + [2, 1]], late, lefts


def split(number, divisor):
    if divisor & (divisor - 1) == 0:
        return number >> (divisor.bit_length() - 1), number & (divisor - 1)
    return lax.div(number, divisor), lax.rem(number, divisor)


def make_plan(sizes, occ, plan):
    row_count, _, slots, tile_rows, tile_cols, room = sizes
    row, col = lax.axis_index("row"), lax.axis_index("col")
    positions = tile_rows * tile_cols
    mine = [occ[col, s, row] for s in range(slots)]
    lines = [split(q, tile_cols) for q in mine]
    lines = [(line * tile_cols, jnp.where(q < positions, c, -1)) for q, (line, c) in zip(mine, lines)]
    ends = [jnp.int32(s * room + 1) for s in range(slots)]
    early, late = column_order(row_count)
    for at, offset in enumerate(early + late):
        tile = row ^ offset
        for u in range(slots):
            q = occ[col, u, tile]
            line, column = split(q, tile_cols)
            panel, depth = split(tile * tile_rows + jnp.minimum(line, tile_rows - 1), tile_cols)
            column = jnp.where(q < positions, column, -2)
            base = (panel ^ col) * slots
            held = [occ[panel, v, row] for v in range(slots)]
            for s in range(slots):
                wanted = jnp.where(lines[s][1] == column, lines[s][0] + depth, -1)
                place = base
                hit = held[0] == wanted
                for v in range(1, slots):
                    also = held[v] == wanted
                    place = jnp.where(also, base + v, place)
                    hit = hit | also
                plan[ends[s]] = place
                plan[ends[s] + 1] = jnp.int32(at * slots + u)
                ends[s] = ends[s] + jnp.where(hit, 2, 0)
    for s in range(slots):
        plan[s * room] = (ends[s] - (s * room + 1)) >> 1
        plan[(s + 1) * room - 1] = (mine[s] < positions).astype(jnp.int32)
        plan[ends[s]] = jnp.int32(0)
        plan[ends[s] + 1] = jnp.int32(0)


def pair_sums(plan, room, left, right, slots):
    counts = [plan[s * room] for s in range(slots)]
    most = functools.reduce(jnp.maximum, counts)
    zero_block = left.shape[0] - 1
    last = right.shape[0] - 1

    def step(turn, totals):
        result = []
        for s in range(slots):
            lefts, rights = [], []
            for half in range(2):
                at = 2 * turn + half
                live = at < counts[s]
                at = s * room + 1 + 2 * jnp.minimum(at, counts[s])
                place, other = plan[at], plan[at + 1]
                live = live & (place < zero_block) & (other <= last)
                lefts.append(left[jnp.where(live, place, zero_block)])
                rights.append(right[jnp.minimum(other, last)])
            product = jnp.dot(
                jnp.concatenate(lefts, axis=1),
                jnp.concatenate(rights, axis=0),
                preferred_element_type=jnp.float32,
            )
            result.append(totals[s] + product)
        return tuple(result)

    block = right.shape[-1]
    zeros = tuple(jnp.zeros((block, block), jnp.float32) for _ in range(slots))
    return lax.fori_loop(0, (most + 1) // 2, step, zeros)


def stack(target, tiles):
    at = 0
    for tile in tiles:
        target[at : at + tile.shape[0]] = tile[...]
        at += tile.shape[0]


def early_square_kernel(sizes, early_count, *refs):
    slots, room = sizes[2], sizes[5]
    occ = refs[0]
    rights = refs[1 : 1 + early_count]
    lefts = (rights[0],) + refs[1 + early_count : -5]
    plan, partial, factors, left, right = refs[-5:]
    block = right.shape[-1]
    stack(right, rights)
    stack(left, lefts)
    left[left.shape[0] - 1] = jnp.zeros(left.shape[1:], left.dtype)
    factors[...] = jnp.zeros(factors.shape, factors.dtype)
    make_plan(sizes, occ, plan)
    sums = pair_sums(plan, room, left, right, slots)
    for s in range(slots):
        partial[s] = sums[s]

        def place(turn, carry, s=s):
            at = s * room + 1 + 2 * turn
            to = jnp.maximum(plan[at + 1] - right.shape[0], -1) + 1
            factors[to, s * block : (s + 1) * block, :] = left[plan[at]]
            return carry

        lax.fori_loop(0, plan[s * room], place, 0)


def late_square_kernel(sizes, factor, *refs):
    slots = sizes[2]
    partial, factors = refs[:2]
    rights = refs[2:-1]
    out = refs[-1]
    block = out.shape[-1]
    left = jnp.concatenate([factors[k] for k in range(1, factors.shape[0])], axis=1)
    right = jnp.concatenate([tile[u] for tile in rights for u in range(tile.shape[0])], axis=0)
    product = jnp.dot(left, right, preferred_element_type=jnp.float32)
    for s in range(slots):
        out[s] = (factor * (partial[s] + product[s * block : (s + 1) * block])).astype(out.dtype)


def early_cube_kernel(sizes, factor, right_count, *refs):
    slots, room = sizes[2], sizes[5]
    plan_in = refs[0]
    rights = refs[1 : 1 + right_count]
    lefts = refs[1 + right_count : 3 + right_count]
    square, partial, factors, left, right, plan, sem, square_sem = refs[3 + right_count :]
    square_copy = pltpu.make_async_copy(lefts[0], square, square_sem)
    square_copy.start()
    copy = pltpu.make_async_copy(plan_in, plan, sem)
    copy.start()
    early = len(lefts) * slots
    block = right.shape[-1]
    stack(right, rights)
    stack(left, lefts)
    left[early] = jnp.zeros(left.shape[1:], left.dtype)
    factors[...] = jnp.zeros(factors.shape, factors.dtype)
    copy.wait()
    sums = pair_sums(plan, room, left, right, slots)
    for s in range(slots):
        stored = plan[(s + 1) * room - 1].astype(jnp.float32)
        own = rights[0][s].astype(jnp.float32) * stored
        partial[s] = 1.5 * own - (0.5 * factor) * sums[s]

        def place(turn, carry, s=s):
            at = s * room + 1 + 2 * turn
            to = jnp.maximum(plan[at] - early, -1) + 1
            factors[to, :, s * block : (s + 1) * block] = right[plan[at + 1]]
            return carry

        lax.fori_loop(0, plan[s * room], place, 0)
    square_copy.wait()


def late_cube_kernel(sizes, factor, *refs):
    slots = sizes[2]
    partial, factors = refs[:2]
    lefts = refs[2:-3]
    updated, result, out_sem = refs[-3:]
    block = result.shape[-1]
    left = jnp.concatenate([tile[u] for tile in lefts for u in range(slots)], axis=1)
    right = factors[1:].reshape(left.shape[1], slots * block)
    product = jnp.dot(left, right, preferred_element_type=jnp.float32)
    copies = []
    for s in range(slots):
        result[s] = partial[s] - (0.5 * factor) * product[:, s * block : (s + 1) * block]
        copies.append(pltpu.make_async_copy(result.at[s], updated.at[s], out_sem.at[s]))
        copies[-1].start()
    for done in copies:
        done.wait()


def per_device(values, occupancy):
    row_count = lax.axis_size("row")
    col_count = lax.axis_size("col")
    slots = values.shape[2]
    block = values.shape[-1]
    tile_rows = RB
    tile_cols = RB * row_count // col_count
    factor = 5.0 / math.sqrt(tile_rows * block * row_count)
    room = 2 * (row_count * slots + 1) + 2
    sizes = (row_count, col_count, slots, tile_rows, tile_cols, room)
    tile = jax.ShapeDtypeStruct((slots, block, block), jnp.bfloat16)
    wide = jax.ShapeDtypeStruct((slots, block, block), jnp.float32)
    dma = pltpu.SemaphoreType.DMA
    plan_shape = ((slots * room,), jnp.int32)

    own = join(values.reshape(tile.shape))
    direct, forwarded, lefts = gather(own, row_count, col_count)
    early_rights = [own] + direct
    late_count = (row_count - len(early_rights)) * slots
    plan, partial, factors = pl.pallas_call(
        functools.partial(early_square_kernel, sizes, len(early_rights)),
        out_shape=(
            jax.ShapeDtypeStruct(*plan_shape),
            wide,
            jax.ShapeDtypeStruct((late_count + 1, slots * block, block), jnp.bfloat16),
        ),
        in_specs=[SMEM] + [VMEM] * (len(early_rights) + len(lefts)),
        out_specs=(SMEM, VMEM, VMEM),
        scratch_shapes=[
            pltpu.VMEM((col_count * slots + 1, block, block), jnp.bfloat16),
            pltpu.VMEM((len(early_rights) * slots, block, block), jnp.bfloat16),
        ],
        compiler_params=PARAMS,
        name="early_square",
    )(occupancy.transpose(1, 2, 0), *early_rights, *lefts)
    square = pl.pallas_call(
        functools.partial(late_square_kernel, sizes, factor),
        out_shape=tile,
        in_specs=[VMEM] * (2 + len(forwarded)),
        out_specs=VMEM,
        compiler_params=PARAMS,
        name="late_square",
    )(partial, factors, *forwarded)

    far = range(2, col_count, 2)
    others = {k: send(square, "col", k) for k in far}
    others[1] = send(square, "col", 1)
    for k in far:
        others[k + 1] = send(others[k], "col", 1)
    rights = early_rights + forwarded
    square_out, partial, factors = pl.pallas_call(
        functools.partial(early_cube_kernel, sizes, factor, len(rights)),
        out_shape=(tile, wide, jax.ShapeDtypeStruct(((col_count - 2) * slots + 1, block, slots * block), jnp.bfloat16)),
        in_specs=[ANY] + [VMEM] * (len(rights) + 2),
        out_specs=(ANY, VMEM, VMEM),
        scratch_shapes=[
            pltpu.VMEM((2 * slots + 1, block, block), jnp.bfloat16),
            pltpu.VMEM((row_count * slots, block, block), jnp.bfloat16),
            pltpu.SMEM(*plan_shape),
            dma,
            dma,
        ],
        compiler_params=PARAMS,
        name="early_cube",
    )(plan, *rights, square, others[1])
    updated = pl.pallas_call(
        functools.partial(late_cube_kernel, sizes, factor),
        out_shape=wide,
        in_specs=[VMEM] * col_count,
        out_specs=ANY,
        scratch_shapes=[pltpu.VMEM(wide.shape, jnp.float32), dma((slots,))],
        compiler_params=PARAMS,
        name="late_cube",
    )(partial, factors, *[others[k] for k in range(2, col_count)])
    shape_out = (1, 1) + tile.shape
    return (square_out.reshape(shape_out), updated.reshape(shape_out))


def solution(mesh):
    spec = P("row", "col", None, None, None)

    return jax.shard_map(
        per_device,
        mesh=mesh,
        in_specs=(spec, P()),
        out_specs=(spec, spec),
        check_vma=False,
    )
```

time: 28.1 us -> 26.6 us (0.947)
  waiting for transfers between devices: 9.73 us -> 8.5 us
  starting transfers between devices: 13 us -> 12.7 us
    ppermute x13 -> x11, waiting for transfers between devices: 9.73 us -> 8.5 us  [send(): return lax.ppermute(array, axis, [(i, i ^ offset) for i in range(size)])]
    ppermute x13 -> x11, starting transfers between devices: 13 us -> 12.7 us  [send(): return lax.ppermute(array, axis, [(i, i ^ offset) for i in range(size)])]
    pallas_call x4 -> x7, Pallas kernels: 3.71 us -> 3.75 us  [the longest x1 1.81 us: per_device(): pl.pallas_call(functools.partial(early_square_kernel, sizes, len(early_ri...]
  transfers between devices with their start and end apart: 13 -> 11, of which waited for: 5 -> 6; matrix products, arithmetic and copies ran while one was open for 0% -> 0% of each run, Pallas kernels for 5% -> 10%
where the time goes in v1:
time: 26.6 us; the launch traced here: 26.5 us
  starting transfers between devices  12.7 us (48%)
  waiting for transfers between devices  8.5 us (32%)
  Pallas kernels  3.75 us (14%)
  local copies, waits for them, and re-layouts  0.84 us (3%)
  between operations  0.7 us (3%)
    ppermute x11, starting transfers between devices, send(): return lax.ppermute(array, axis, [(i, i ^ offset) for i in range(size)])  12.7 us
    ppermute x11, waiting for transfers between devices, send(): return lax.ppermute(array, axis, [(i, i ^ offset) for i in range(size)])  8.5 us
    pallas_call x1, Pallas kernels, per_device(): pl.pallas_call(functools.partial(early_square_kernel, sizes, len(early_ri...  1.81 us
    pallas_call x1, Pallas kernels, per_device(): pl.pallas_call(functools.partial(late_cube_kernel, sizes, factor), out_sh...  0.86 us
    unnamed x4, local copies, waits for them, and re-layouts  0.84 us
    pallas_call x1, Pallas kernels, per_device(): pl.pallas_call(functools.partial(early_cube_kernel, sizes, factor, len(ri...  0.81 us
  transfers between devices with their start and end apart: 11, of which 6 were waited for; matrix products, arithmetic and copies ran while one was open for 0% of the time, Pallas kernels for 10%

profile of v1, /device:TPU:0, one launch (start us, length us, event | category | flops | bytes accessed | tf_op | source)
XLA Modules:
  0.0 26.5 jit_solution(24350284098784398)
XLA Ops:
  0.6 0.0 copy-start
  0.6 0.8 %copy-done = bf16[1,1,2,128,128]{4,3,2,1,0:T(8,128)(2,1)S(1)} copy-done((bf16[1,1,2,128,128]{4,3,2,1,0:T(8,128)(2,1)S(1)}, bf16[1,1,2,128,128]{4,3,2,1,0:T(8,128)(2,1)}, u32[]{:S(2)}) %copy-start) | copy-done | bytes 65560
  1.5 0.5 %collective-permute-start.4 = (bf16[2,128,128]{2,1,0:T(8,128)(2,1)S(1)}, bf16[2,128,128]{2,1,0:T(8,128)(2,1)S(1)}, u32[]{:S(2)}, u32[]{:S(2)}) collective-permute-start(bf16[2,128,128]{2,1,0:T(8,128)(2,1)S(1)} %join.3.refs_0_.refs_1_), channel_id=1, source_target_pairs={{0,1},{1,0},{2,3},{3,2},{4,5},{5,4},{6,7},{7,6},{8,9},{9,8},{10,11... | collective-permute-start | bytes 196616 | tf_op jit(solution)/shard_map/ppermute | solution.py:21
  2.0 4.7 %collective-permute-start = (bf16[2,128,128]{2,1,0:T(8,128)(2,1)S(1)}, bf16[2,128,128]{2,1,0:T(8,128)(2,1)S(1)}, u32[]{:S(2)}, u32[]{:S(2)}) collective-permute-start(bf16[2,128,128]{2,1,0:T(8,128)(2,1)S(1)} %join.3.refs_0_.refs_1_), channel_id=1, source_target_pairs={{0,24},{4,28},{8,16},{12,20},{16,8},{20,12},{24,0},{28,4},{1,25},{... | collective-permute-start | bytes 196616 | tf_op jit(solution)/shard_map/ppermute | solution.py:21
  6.6 0.0 collective-permute-start.2
  6.6 0.0 collective-permute-done.4.refs_1_.refs_6_
  6.6 1.6 %collective-permute-start.5 = (bf16[4,128,128]{2,1,0:T(8,128)(2,1)S(1)}, bf16[4,128,128]{2,1,0:T(8,128)(2,1)S(1)}, u32[]{:S(2)}, u32[]{:S(2)}) collective-permute-start(bf16[4,128,128]{2,1,0:T(8,128)(2,1)S(1)} %join.4), channel_id=1, source_target_pairs={{0,2},{1,3},{2,0},{3,1},{4,6},{5,7},{6,4},{7,5},{8,10},{9,11},{10,... | collective-permute-start | bytes 393224 | tf_op jit(solution)/shard_map/ppermute | solution.py:21
  8.2 0.8 %collective-permute-start.1 = (bf16[2,128,128]{2,1,0:T(8,128)(2,1)S(1)}, bf16[2,128,128]{2,1,0:T(8,128)(2,1)S(1)}, u32[]{:S(2)}, u32[]{:S(2)}) collective-permute-start(bf16[2,128,128]{2,1,0:T(8,128)(2,1)S(1)} %join.3.refs_0_.refs_1_), channel_id=1, source_target_pairs={{0,16},{4,20},{8,24},{12,28},{16,0},{20,4},{24,8},{28,12},{1,17},{... | collective-permute-start | bytes 196616 | tf_op jit(solution)/shard_map/ppermute | solution.py:21
  9.0 0.6 %collective-permute-done.refs_2_.refs_1_ = bf16[2,128,128]{2,1,0:T(8,128)(2,1)S(1)} collective-permute-done((bf16[2,128,128]{2,1,0:T(8,128)(2,1)S(1)}, bf16[2,128,128]{2,1,0:T(8,128)(2,1)S(1)}, u32[]{:S(2)}, u32[]{:S(2)}) %collective-permute-start) | collective-permute-done | bytes 65568 | tf_op jit(solution)/shard_map/ppermute | solution.py:21
  9.6 1.3 %collective-permute-done.2.refs_4_.refs_0_ = bf16[2,128,128]{2,1,0:T(8,128)(2,1)S(1)} collective-permute-done((bf16[2,128,128]{2,1,0:T(8,128)(2,1)S(1)}, bf16[2,128,128]{2,1,0:T(8,128)(2,1)S(1)}, u32[]{:S(2)}, u32[]{:S(2)}) %collective-permute-start.2) | collective-permute-done | bytes 65568 | tf_op jit(solution)/shard_map/ppermute | solution.py:21
  10.9 0.0 copy-start.1
  10.9 1.6 %collective-permute-start.6 = (bf16[4,128,128]{2,1,0:T(8,128)(2,1)S(1)}, bf16[4,128,128]{2,1,0:T(8,128)(2,1)S(1)}, u32[]{:S(2)}, u32[]{:S(2)}) collective-permute-start(bf16[4,128,128]{2,1,0:T(8,128)(2,1)S(1)} %join.5), channel_id=1, source_target_pairs={{0,4},{4,0},{8,12},{12,8},{16,20},{20,16},{24,28},{28,24},{1,5},{5... | collective-permute-start | bytes 393224 | tf_op jit(solution)/shard_map/ppermute | solution.py:21
  12.6 0.4 %collective-permute-start.3 = (bf16[2,128,128]{2,1,0:T(8,128)(2,1)S(1)}, bf16[2,128,128]{2,1,0:T(8,128)(2,1)S(1)}, u32[]{:S(2)}, u32[]{:S(2)}) collective-permute-start(bf16[2,128,128]{2,1,0:T(8,128)(2,1)S(1)} %join.3.refs_0_.refs_1_), channel_id=1, source_target_pairs={{0,4},{4,0},{8,12},{12,8},{16,20},{20,16},{24,28},{28,24},{1,5},{5... | collective-permute-start | bytes 196616 | tf_op jit(solution)/shard_map/ppermute | solution.py:21
  13.0 1.1 %collective-permute-done.1.refs_3_ = bf16[2,128,128]{2,1,0:T(8,128)(2,1)S(1)} collective-permute-done((bf16[2,128,128]{2,1,0:T(8,128)(2,1)S(1)}, bf16[2,128,128]{2,1,0:T(8,128)(2,1)S(1)}, u32[]{:S(2)}, u32[]{:S(2)}) %collective-permute-start.1) | collective-permute-done | bytes 65568 | tf_op jit(solution)/shard_map/ppermute | solution.py:21
  14.1 1.5 %collective-permute-start.7 = (bf16[2,128,128]{2,1,0:T(8,128)(2,1)S(1)}, bf16[2,128,128]{2,1,0:T(8,128)(2,1)S(1)}, u32[]{:S(2)}, u32[]{:S(2)}) collective-permute-start(bf16[2,128,128]{2,1,0:T(8,128)(2,1)S(1)} %collective-permute-done.1.refs_3_), channel_id=1, source_target_pairs={{0,4},{4,0},{8,12},{12,8},{16,20},{20,16},{24,28},{28,24},{1,5},{5... | collective-permute-start | bytes 196616 | tf_op jit(solution)/shard_map/ppermute | solution.py:21
  15.6 2.3 %collective-permute-done.3.refs_5_ = bf16[2,128,128]{2,1,0:T(8,128)(2,1)S(1)} collective-permute-done((bf16[2,128,128]{2,1,0:T(8,128)(2,1)S(1)}, bf16[2,128,128]{2,1,0:T(8,128)(2,1)S(1)}, u32[]{:S(2)}, u32[]{:S(2)}) %collective-permute-start.3) | collective-permute-done | bytes 65568 | tf_op jit(solution)/shard_map/ppermute | solution.py:21
  17.9 0.0 collective-permute-done.5.refs_7_
  17.9 0.0 copy-done.1
  17.9 1.8 %early_square.1 = (s32[72]{0:T(128)S(1)}, f32[2,128,128]{2,1,0:T(8,128)S(1)}, bf16[7,256,128]{2,1,0:T(8,128)(2,1)S(1)}) custom-call(s32[4,2,8]{2,1,0:T(2,128)S(1)} %bitcast.5, bf16[2,128,128]{2,1,0:T(8,128)(2,1)S(1)} %join.3.refs_0_.refs_1_, bf16[2,128,128]{2,1,0:T(8,128)(2,1)S(1)} %collective-permute-done.refs_2_.refs_1_, ...), custom_call_target="tpu_custom_call" | custom-call | tf_op jit(solution)/shard_map/early_square/pallas_call | solution.py:254
  19.7 0.0 collective-permute-done.7.refs_3_.refs_7_
  19.7 0.0 collective-permute-done.6.refs_2_.refs_6_
  19.8 0.2 late_square.1.refs_8_
  20.0 1.6 %collective-permute-start.9 = (bf16[2,128,128]{2,1,0:T(8,128)(2,1)S(1)}, bf16[2,128,128]{2,1,0:T(8,128)(2,1)S(1)}, u32[]{:S(2)}, u32[]{:S(2)}) collective-permute-start(bf16[2,128,128]{2,1,0:T(8,128)(2,1)S(1)} %late_square.1.refs_8_), channel_id=1, source_target_pairs={{0,2},{1,3},{2,0},{3,1},{4,6},{5,7},{6,4},{7,5},{8,10},{9,11},{10,... | collective-permute-start | bytes 196616 | tf_op jit(solution)/shard_map/ppermute | solution.py:21
  21.6 0.0 collective-permute-start.8
  21.6 2.8 %collective-permute-done.9.refs_2_ = bf16[2,128,128]{2,1,0:T(8,128)(2,1)S(1)} collective-permute-done((bf16[2,128,128]{2,1,0:T(8,128)(2,1)S(1)}, bf16[2,128,128]{2,1,0:T(8,128)(2,1)S(1)}, u32[]{:S(2)}, u32[]{:S(2)}) %collective-permute-start.9) | collective-permute-done | bytes 65568 | tf_op jit(solution)/shard_map/ppermute | solution.py:21
  24.3 0.0 collective-permute-start.10
  24.3 0.0 collective-permute-done.8.refs_9_
  24.4 0.8 %early_cube.1 = (bf16[2,128,128]{2,1,0:T(8,128)(2,1)}, f32[2,128,128]{2,1,0:T(8,128)S(1)}, bf16[5,128,256]{2,1,0:T(8,128)(2,1)S(1)}) custom-call(s32[72]{0:T(128)S(1)} %get-tuple-element.8.refs_0_, bf16[2,128,128]{2,1,0:T(8,128)(2,1)S(1)} %join.3.refs_0_.refs_1_, bf16[2,128,128]{2,1,0:T(8,128)(2,1)S(1)} %collective-permute-done.refs_2_.refs_1_, ...), custom_call_target="tpu_custom_call" | custom-call | tf_op jit(solution)/shard_map/early_cube/pallas_call | solution.py:285
  25.2 0.4 %collective-permute-done.10.refs_3_ = bf16[2,128,128]{2,1,0:T(8,128)(2,1)S(1)} collective-permute-done((bf16[2,128,128]{2,1,0:T(8,128)(2,1)S(1)}, bf16[2,128,128]{2,1,0:T(8,128)(2,1)S(1)}, u32[]{:S(2)}, u32[]{:S(2)}) %collective-permute-start.10) | collective-permute-done | bytes 65568 | tf_op jit(solution)/shard_map/ppermute | solution.py:21
  25.6 0.9 %late_cube.1 = f32[2,128,128]{2,1,0:T(8,128)} custom-call(f32[2,128,128]{2,1,0:T(8,128)S(1)} %get-tuple-element.12.refs_0_, bf16[5,128,256]{2,1,0:T(8,128)(2,1)S(1)} %get-tuple-element.13.refs_1_, bf16[2,128,128]{2,1,0:T(8,128)(2,1)S(1)} %collective-permute-done.9.refs_2_, bf16[2,128,128]{2,1,0:T(8,128)(2,1)S(1)} %collective-permute-done.10.refs_3_), custom_call_target="tpu_custom_call" | custom-call | tf_op jit(solution)/shard_map/late_cube/pallas_call | solution.py:300
  (3 shorter events, 0.0 us)
Async XLA Ops:
  0.6 0.8 %copy-start = (bf16[1,1,2,128,128]{4,3,2,1,0:T(8,128)(2,1)S(1)}, bf16[1,1,2,128,128]{4,3,2,1,0:T(8,128)(2,1)}, u32[]{:S(2)}) copy-start(bf16[1,1,2,128,128]{4,3,2,1,0:T(8,128)(2,1)} %param.2) | copy-start | bytes 196612
  1.5 5.2 %collective-permute-start.4 = (bf16[2,128,128]{2,1,0:T(8,128)(2,1)S(1)}, bf16[2,128,128]{2,1,0:T(8,128)(2,1)S(1)}, u32[]{:S(2)}, u32[]{:S(2)}) collective-permute-start(bf16[2,128,128]{2,1,0:T(8,128)(2,1)S(1)} %join.3.refs_0_.refs_1_), channel_id=1, source_target_pairs={{0,1},{1,0},{2,3},{3,2},{4,5},{5,4},{6,7},{7,6},{8,9},{9,8},{10,11... | collective-permute-start | bytes 196616 | tf_op jit(solution)/shard_map/ppermute | solution.py:21
  2.0 7.7 %collective-permute-start = (bf16[2,128,128]{2,1,0:T(8,128)(2,1)S(1)}, bf16[2,128,128]{2,1,0:T(8,128)(2,1)S(1)}, u32[]{:S(2)}, u32[]{:S(2)}) collective-permute-start(bf16[2,128,128]{2,1,0:T(8,128)(2,1)S(1)} %join.3.refs_0_.refs_1_), channel_id=1, source_target_pairs={{0,24},{4,28},{8,16},{12,20},{16,8},{20,12},{24,0},{28,4},{1,25},{... | collective-permute-start | bytes 196616 | tf_op jit(solution)/shard_map/ppermute | solution.py:21
  6.6 4.3 %collective-permute-start.2 = (bf16[2,128,128]{2,1,0:T(8,128)(2,1)S(1)}, bf16[2,128,128]{2,1,0:T(8,128)(2,1)S(1)}, u32[]{:S(2)}, u32[]{:S(2)}) collective-permute-start(bf16[2,128,128]{2,1,0:T(8,128)(2,1)S(1)} %join.3.refs_0_.refs_1_), channel_id=1, source_target_pairs={{0,8},{4,12},{8,0},{12,4},{16,24},{20,28},{24,16},{28,20},{1,9},{5... | collective-permute-start | bytes 196616 | tf_op jit(solution)/shard_map/ppermute | solution.py:21
  6.6 11.3 %collective-permute-start.5 = (bf16[4,128,128]{2,1,0:T(8,128)(2,1)S(1)}, bf16[4,128,128]{2,1,0:T(8,128)(2,1)S(1)}, u32[]{:S(2)}, u32[]{:S(2)}) collective-permute-start(bf16[4,128,128]{2,1,0:T(8,128)(2,1)S(1)} %join.4), channel_id=1, source_target_pairs={{0,2},{1,3},{2,0},{3,1},{4,6},{5,7},{6,4},{7,5},{8,10},{9,11},{10,... | collective-permute-start | bytes 393224 | tf_op jit(solution)/shard_map/ppermute | solution.py:21
  8.2 5.9 %collective-permute-start.1 = (bf16[2,128,128]{2,1,0:T(8,128)(2,1)S(1)}, bf16[2,128,128]{2,1,0:T(8,128)(2,1)S(1)}, u32[]{:S(2)}, u32[]{:S(2)}) collective-permute-start(bf16[2,128,128]{2,1,0:T(8,128)(2,1)S(1)} %join.3.refs_0_.refs_1_), channel_id=1, source_target_pairs={{0,16},{4,20},{8,24},{12,28},{16,0},{20,4},{24,8},{28,12},{1,17},{... | collective-permute-start | bytes 196616 | tf_op jit(solution)/shard_map/ppermute | solution.py:21
  10.9 7.0 %copy-start.1 = (s32[8,4,2]{0,2,1:T(2,128)S(1)}, s32[8,4,2]{0,2,1:T(2,128)}, u32[]{:S(2)}) copy-start(s32[8,4,2]{0,2,1:T(2,128)} %param.3) | copy-start | bytes 772
  10.9 8.8 %collective-permute-start.6 = (bf16[4,128,128]{2,1,0:T(8,128)(2,1)S(1)}, bf16[4,128,128]{2,1,0:T(8,128)(2,1)S(1)}, u32[]{:S(2)}, u32[]{:S(2)}) collective-permute-start(bf16[4,128,128]{2,1,0:T(8,128)(2,1)S(1)} %join.5), channel_id=1, source_target_pairs={{0,4},{4,0},{8,12},{12,8},{16,20},{20,16},{24,28},{28,24},{1,5},{5... | collective-permute-start | bytes 393224 | tf_op jit(solution)/shard_map/ppermute | solution.py:21
  12.6 5.3 %collective-permute-start.3 = (bf16[2,128,128]{2,1,0:T(8,128)(2,1)S(1)}, bf16[2,128,128]{2,1,0:T(8,128)(2,1)S(1)}, u32[]{:S(2)}, u32[]{:S(2)}) collective-permute-start(bf16[2,128,128]{2,1,0:T(8,128)(2,1)S(1)} %join.3.refs_0_.refs_1_), channel_id=1, source_target_pairs={{0,4},{4,0},{8,12},{12,8},{16,20},{20,16},{24,28},{28,24},{1,5},{5... | collective-permute-start | bytes 196616 | tf_op jit(solution)/shard_map/ppermute | solution.py:21
  14.1 5.6 %collective-permute-start.7 = (bf16[2,128,128]{2,1,0:T(8,128)(2,1)S(1)}, bf16[2,128,128]{2,1,0:T(8,128)(2,1)S(1)}, u32[]{:S(2)}, u32[]{:S(2)}) collective-permute-start(bf16[2,128,128]{2,1,0:T(8,128)(2,1)S(1)} %collective-permute-done.1.refs_3_), channel_id=1, source_target_pairs={{0,4},{4,0},{8,12},{12,8},{16,20},{20,16},{24,28},{28,24},{1,5},{5... | collective-permute-start | bytes 196616 | tf_op jit(solution)/shard_map/ppermute | solution.py:21
  20.0 4.3 %collective-permute-start.9 = (bf16[2,128,128]{2,1,0:T(8,128)(2,1)S(1)}, bf16[2,128,128]{2,1,0:T(8,128)(2,1)S(1)}, u32[]{:S(2)}, u32[]{:S(2)}) collective-permute-start(bf16[2,128,128]{2,1,0:T(8,128)(2,1)S(1)} %late_square.1.refs_8_), channel_id=1, source_target_pairs={{0,2},{1,3},{2,0},{3,1},{4,6},{5,7},{6,4},{7,5},{8,10},{9,11},{10,... | collective-permute-start | bytes 196616 | tf_op jit(solution)/shard_map/ppermute | solution.py:21
  21.6 2.8 %collective-permute-start.8 = (bf16[2,128,128]{2,1,0:T(8,128)(2,1)S(1)}, bf16[2,128,128]{2,1,0:T(8,128)(2,1)S(1)}, u32[]{:S(2)}, u32[]{:S(2)}) collective-permute-start(bf16[2,128,128]{2,1,0:T(8,128)(2,1)S(1)} %late_square.1.refs_8_), channel_id=1, source_target_pairs={{0,1},{1,0},{2,3},{3,2},{4,5},{5,4},{6,7},{7,6},{8,9},{9,8},{10,11... | collective-permute-start | bytes 196616 | tf_op jit(solution)/shard_map/ppermute | solution.py:21
  24.3 1.3 %collective-permute-start.10 = (bf16[2,128,128]{2,1,0:T(8,128)(2,1)S(1)}, bf16[2,128,128]{2,1,0:T(8,128)(2,1)S(1)}, u32[]{:S(2)}, u32[]{:S(2)}) collective-permute-start(bf16[2,128,128]{2,1,0:T(8,128)(2,1)S(1)} %collective-permute-done.9.refs_2_), channel_id=1, source_target_pairs={{0,1},{1,0},{2,3},{3,2},{4,5},{5,4},{6,7},{7,6},{8,9},{9,8},{10,11... | collective-permute-start | bytes 196616 | tf_op jit(solution)/shard_map/ppermute | solution.py:21

commit v2 on v1

--- a/solution.py
+++ b/solution.py
@@ -41,26 +41,34 @@
 
 
 def far_rows(row_count):
-    return list(range(row_count - 2, 2, -2))
+    return list(range(row_count - 4, 0, -4))
 
 
 def column_order(row_count):
     far = far_rows(row_count)
-    early = [0] + far + [2, 1]
-    late = [3] + [k + 1 for k in far]
+    early = [0] + [g + 2 for g in far] + [2, 1] + [g + 1 for g in far]
+    late = [3, far[0] + 3, far[0]]
+    for g in far[1:]:
+        late += [g + 3, g]
     return early, late
 
 
-def gather(own, row_count, col_count):
+def gather(values, row_count, col_count):
     far = far_rows(row_count)
-    rows = {k: send(own, "row", k) for k in far + [2]}
-    near = send(own, "col", 1)
-    rows[1] = send(own, "row", 1)
+    rows = {k: send(values, "row", k) for k in [g + 2 for g in far] + [2]}
+    near = send(values, "col", 1)
+    for k in [1] + [g + 1 for g in far]:
+        rows[k] = send(values, "row", k)
+    direct = list(rows.values())
+    own = join(values)
     pair = join(own, near)
     lefts = [near] + [send(pair, "col", k) for k in range(2, col_count, 2)]
-    late = [send(join(rows[2], rows[far[0]]), "row", 1)]
-    late += [send(rows[k], "row", 1) for k in far[1:]]
-    return [rows[k] for k in far + [2, 1]], late, lefts
+    late = []
+    for g in far:
+        source = rows[g + 2]
+        late.append(send(source if late else join(rows[2], source), "row", 1))
+        late.append(send(source, "row", 2))
+    return own, direct, late, lefts
 
 
 def split(number, divisor):
@@ -69,7 +77,7 @@
     return lax.div(number, divisor), lax.rem(number, divisor)
 
 
-def make_plan(sizes, occ, plan):
+def plan_kernel(sizes, occ, plan):
     row_count, _, slots, tile_rows, tile_cols, room = sizes
     row, col = lax.axis_index("row"), lax.axis_index("col")
     positions = tile_rows * tile_cols
@@ -145,16 +153,17 @@
 
 def early_square_kernel(sizes, early_count, *refs):
     slots, room = sizes[2], sizes[5]
-    occ = refs[0]
     rights = refs[1 : 1 + early_count]
-    lefts = (rights[0],) + refs[1 + early_count : -5]
-    plan, partial, factors, left, right = refs[-5:]
+    lefts = (rights[0],) + refs[1 + early_count : -6]
+    partial, factors, left, right, plan, sem = refs[-6:]
     block = right.shape[-1]
+    copy = pltpu.make_async_copy(refs[0], plan, sem)
+    copy.start()
     stack(right, rights)
     stack(left, lefts)
     left[left.shape[0] - 1] = jnp.zeros(left.shape[1:], left.dtype)
     factors[...] = jnp.zeros(factors.shape, factors.dtype)
-    make_plan(sizes, occ, plan)
+    copy.wait()
     sums = pair_sums(plan, room, left, right, slots)
     for s in range(slots):
         partial[s] = sums[s]
@@ -247,26 +256,31 @@
     dma = pltpu.SemaphoreType.DMA
     plan_shape = ((slots * room,), jnp.int32)
 
-    own = join(values.reshape(tile.shape))
-    direct, forwarded, lefts = gather(own, row_count, col_count)
+    own, direct, forwarded, lefts = gather(values.reshape(tile.shape), row_count, col_count)
     early_rights = [own] + direct
     late_count = (row_count - len(early_rights)) * slots
-    plan, partial, factors = pl.pallas_call(
+    plan = pl.pallas_call(
+        functools.partial(plan_kernel, sizes),
+        out_shape=jax.ShapeDtypeStruct(*plan_shape),
+        in_specs=[SMEM],
+        out_specs=SMEM,
+        compiler_params=PARAMS,
+        name="plan",
+    )(occupancy.transpose(1, 2, 0))
+    partial, factors = pl.pallas_call(
         functools.partial(early_square_kernel, sizes, len(early_rights)),
-        out_shape=(
-            jax.ShapeDtypeStruct(*plan_shape),
-            wide,
-            jax.ShapeDtypeStruct((late_count + 1, slots * block, block), jnp.bfloat16),
-        ),
-        in_specs=[SMEM] + [VMEM] * (len(early_rights) + len(lefts)),
-        out_specs=(SMEM, VMEM, VMEM),
+        out_shape=(wide, jax.ShapeDtypeStruct((late_count + 1, slots * block, block), jnp.bfloat16)),
+        in_specs=[ANY] + [VMEM] * (len(early_rights) + len(lefts)),
+        out_specs=(VMEM, VMEM),
         scratch_shapes=[
             pltpu.VMEM((col_count * slots + 1, block, block), jnp.bfloat16),
             pltpu.VMEM((len(early_rights) * slots, block, block), jnp.bfloat16),
+            pltpu.SMEM(*plan_shape),
+            dma,
         ],
         compiler_params=PARAMS,
         name="early_square",
-    )(occupancy.transpose(1, 2, 0), *early_rights, *lefts)
+    )(plan, *early_rights, *lefts)
     square = pl.pallas_call(
         functools.partial(late_square_kernel, sizes, factor),
         out_shape=tile,

time: 26.6 us -> 26.5 us (level)
  waiting for transfers between devices: 8.5 us -> 6.13 us
  starting transfers between devices: 12.7 us -> 14.4 us
  Pallas kernels: 3.75 us -> 5.12 us
  local copies, waits for them, and re-layouts: 0.84 us -> 0.01 us
    ppermute x11, waiting for transfers between devices: 8.5 us -> 6.13 us  [send(): return lax.ppermute(array, axis, [(i, i ^ offset) for i in range(size)])]
    ppermute x11, starting transfers between devices: 12.7 us -> 14.4 us  [send(): return lax.ppermute(array, axis, [(i, i ^ offset) for i in range(size)])]
    pallas_call x0 -> x1, Pallas kernels: none -> 1.5 us  [per_device(): pl.pallas_call(functools.partial(plan_kernel, sizes), out_shape=jax.Shape...]
    pallas_call x1, Pallas kernels: 1.81 us -> 0.78 us  [per_device(): pl.pallas_call(functools.partial(early_square_kernel, sizes, len(early_ri...]
    pallas_call x3, Pallas kernels: 0.02 us -> 0.93 us  [join(): pl.pallas_call(join_kernel, out_shape=jax.ShapeDtypeStruct(shape, arrays[...]
    unnamed x4 -> x2, local copies, waits for them, and re-layouts: 0.84 us -> 0.01 us
  transfers between devices with their start and end apart: 11 -> 11, of which waited for: 6 -> 5; matrix products, arithmetic and copies ran while one was open for 0% -> 0% of each run, Pallas kernels for 10% -> 15%
where the time goes in v2:
time: 26.5 us; the launch traced here: 26.3 us
  starting transfers between devices  14.4 us (54%)
  waiting for transfers between devices  6.13 us (23%)
  Pallas kernels  5.12 us (19%)
  between operations  0.7 us (3%)
    ppermute x11, starting transfers between devices, send(): return lax.ppermute(array, axis, [(i, i ^ offset) for i in range(size)])  14.4 us
    ppermute x11, waiting for transfers between devices, send(): return lax.ppermute(array, axis, [(i, i ^ offset) for i in range(size)])  6.13 us
    pallas_call x1, Pallas kernels, per_device(): pl.pallas_call(functools.partial(plan_kernel, sizes), out_shape=jax.Shape...  1.5 us
    pallas_call x3, Pallas kernels, join(): pl.pallas_call(join_kernel, out_shape=jax.ShapeDtypeStruct(shape, arrays[...  0.93 us
    pallas_call x1, Pallas kernels, per_device(): pl.pallas_call(functools.partial(late_cube_kernel, sizes, factor), out_sh...  0.86 us
    pallas_call x1, Pallas kernels, per_device(): pl.pallas_call(functools.partial(early_cube_kernel, sizes, factor, len(ri...  0.81 us
    pallas_call x1, Pallas kernels, per_device(): pl.pallas_call(functools.partial(early_square_kernel, sizes, len(early_ri...  0.78 us
  transfers between devices with their start and end apart: 11, of which 5 were waited for; matrix products, arithmetic and copies ran while one was open for 0% of the time, Pallas kernels for 15%

profile of v2, /device:TPU:0, one launch (start us, length us, event | category | flops | bytes accessed | tf_op | source)
XLA Modules:
  0.0 26.3 jit_solution(458837700089785165)
XLA Ops:
  0.6 0.6 %collective-permute-start.6 = (bf16[2,128,128]{2,1,0:T(8,128)(2,1)}, bf16[2,128,128]{2,1,0:T(8,128)(2,1)S(1)}, u32[]{:S(2)}, u32[]{:S(2)}) collective-permute-start(bf16[2,128,128]{2,1,0:T(8,128)(2,1)} %bitcast.1.refs_0_), channel_id=1, source_target_pairs={{0,1},{1,0},{2,3},{3,2},{4,5},{5,4},{6,7},{7,6},{8,9},{9,8},{10,11... | collective-permute-start | bytes 196616 | tf_op jit(solution)/shard_map/ppermute | solution.py:21
  1.2 4.7 %collective-permute-start = (bf16[2,128,128]{2,1,0:T(8,128)(2,1)}, bf16[2,128,128]{2,1,0:T(8,128)(2,1)S(1)}, u32[]{:S(2)}, u32[]{:S(2)}) collective-permute-start(bf16[2,128,128]{2,1,0:T(8,128)(2,1)} %bitcast.1.refs_0_), channel_id=1, source_target_pairs={{0,24},{4,28},{8,16},{12,20},{16,8},{20,12},{24,0},{28,4},{1,25},{... | collective-permute-start | bytes 196616 | tf_op jit(solution)/shard_map/ppermute | solution.py:21
  5.9 0.0 collective-permute-start.1
  5.9 0.9 %join.3.refs_0_.refs_1_ = bf16[2,128,128]{2,1,0:T(8,128)(2,1)S(1)} custom-call(bf16[2,128,128]{2,1,0:T(8,128)(2,1)} %bitcast.1.refs_0_), custom_call_target="tpu_custom_call" | custom-call | tf_op jit(solution)/shard_map/join/pallas_call | solution.py:33
  6.8 0.0 collective-permute-done.6.refs_1_.refs_6_
  6.8 1.6 %collective-permute-start.7 = (bf16[4,128,128]{2,1,0:T(8,128)(2,1)S(1)}, bf16[4,128,128]{2,1,0:T(8,128)(2,1)S(1)}, u32[]{:S(2)}, u32[]{:S(2)}) collective-permute-start(bf16[4,128,128]{2,1,0:T(8,128)(2,1)S(1)} %join.5), channel_id=1, source_target_pairs={{0,2},{1,3},{2,0},{3,1},{4,6},{5,7},{6,4},{7,5},{8,10},{9,11},{10,... | collective-permute-start | bytes 393224 | tf_op jit(solution)/shard_map/ppermute | solution.py:21
  8.4 0.7 %collective-permute-done.refs_1_.refs_2_ = bf16[2,128,128]{2,1,0:T(8,128)(2,1)S(1)} collective-permute-done((bf16[2,128,128]{2,1,0:T(8,128)(2,1)}, bf16[2,128,128]{2,1,0:T(8,128)(2,1)S(1)}, u32[]{:S(2)}, u32[]{:S(2)}) %collective-permute-start) | collective-permute-done | bytes 65568 | tf_op jit(solution)/shard_map/ppermute | solution.py:21
  9.1 1.3 %collective-permute-done.1.refs_0_.refs_3_ = bf16[2,128,128]{2,1,0:T(8,128)(2,1)S(1)} collective-permute-done((bf16[2,128,128]{2,1,0:T(8,128)(2,1)}, bf16[2,128,128]{2,1,0:T(8,128)(2,1)S(1)}, u32[]{:S(2)}, u32[]{:S(2)}) %collective-permute-start.1) | collective-permute-done | bytes 65568 | tf_op jit(solution)/shard_map/ppermute | solution.py:21
  10.3 0.0 copy-start
  10.4 1.6 %collective-permute-start.4 = (bf16[4,128,128]{2,1,0:T(8,128)(2,1)S(1)}, bf16[4,128,128]{2,1,0:T(8,128)(2,1)S(1)}, u32[]{:S(2)}, u32[]{:S(2)}) collective-permute-start(bf16[4,128,128]{2,1,0:T(8,128)(2,1)S(1)} %join.4), channel_id=1, source_target_pairs={{0,4},{4,0},{8,12},{12,8},{16,20},{20,16},{24,28},{28,24},{1,5},{5... | collective-permute-start | bytes 393224 | tf_op jit(solution)/shard_map/ppermute | solution.py:21
  12.0 0.4 %collective-permute-start.2 = (bf16[2,128,128]{2,1,0:T(8,128)(2,1)}, bf16[2,128,128]{2,1,0:T(8,128)(2,1)S(1)}, u32[]{:S(2)}, u32[]{:S(2)}) collective-permute-start(bf16[2,128,128]{2,1,0:T(8,128)(2,1)} %bitcast.1.refs_0_), channel_id=1, source_target_pairs={{0,4},{4,0},{8,12},{12,8},{16,20},{20,16},{24,28},{28,24},{1,5},{5... | collective-permute-start | bytes 196616 | tf_op jit(solution)/shard_map/ppermute | solution.py:21
  12.4 1.3 %collective-permute-start.3 = (bf16[2,128,128]{2,1,0:T(8,128)(2,1)}, bf16[2,128,128]{2,1,0:T(8,128)(2,1)S(1)}, u32[]{:S(2)}, u32[]{:S(2)}) collective-permute-start(bf16[2,128,128]{2,1,0:T(8,128)(2,1)} %bitcast.1.refs_0_), channel_id=1, source_target_pairs={{0,20},{4,16},{8,28},{12,24},{16,4},{20,0},{24,12},{28,8},{1,21},{... | collective-permute-start | bytes 196616 | tf_op jit(solution)/shard_map/ppermute | solution.py:21
  13.8 2.7 %collective-permute-start.5 = (bf16[2,128,128]{2,1,0:T(8,128)(2,1)S(1)}, bf16[2,128,128]{2,1,0:T(8,128)(2,1)S(1)}, u32[]{:S(2)}, u32[]{:S(2)}) collective-permute-start(bf16[2,128,128]{2,1,0:T(8,128)(2,1)S(1)} %collective-permute-done.refs_1_.refs_2_), channel_id=1, source_target_pairs={{0,8},{4,12},{8,0},{12,4},{16,24},{20,28},{24,16},{28,20},{1,9},{5... | collective-permute-start | bytes 196616 | tf_op jit(solution)/shard_map/ppermute | solution.py:21
  16.4 0.0 copy-done
  16.4 1.5 %plan.1.refs_0_ = s32[72]{0:T(128)S(1)} custom-call(s32[4,2,8]{2,1,0:T(2,128)S(1)} %bitcast.4), custom_call_target="tpu_custom_call" | custom-call | tf_op jit(solution)/shard_map/plan/pallas_call | solution.py:262
  17.9 0.0 collective-permute-done.2.refs_4_
  18.0 0.9 %collective-permute-done.3.refs_5_ = bf16[2,128,128]{2,1,0:T(8,128)(2,1)S(1)} collective-permute-done((bf16[2,128,128]{2,1,0:T(8,128)(2,1)}, bf16[2,128,128]{2,1,0:T(8,128)(2,1)S(1)}, u32[]{:S(2)}, u32[]{:S(2)}) %collective-permute-start.3) | collective-permute-done | bytes 65568 | tf_op jit(solution)/shard_map/ppermute | solution.py:21
  18.8 0.0 collective-permute-done.7.refs_7_
  18.8 0.8 %early_square.1 = (f32[2,128,128]{2,1,0:T(8,128)S(1)}, bf16[7,256,128]{2,1,0:T(8,128)(2,1)S(1)}) custom-call(s32[72]{0:T(128)S(1)} %plan.1.refs_0_, bf16[2,128,128]{2,1,0:T(8,128)(2,1)S(1)} %join.3.refs_0_.refs_1_, bf16[2,128,128]{2,1,0:T(8,128)(2,1)S(1)} %collective-permute-done.refs_1_.refs_2_, ...), custom_call_target="tpu_custom_call" | custom-call | tf_op jit(solution)/shard_map/early_square/pallas_call | solution.py:270
  19.6 0.0 collective-permute-done.5.refs_3_.refs_7_
  19.6 0.0 collective-permute-done.4.refs_2_.refs_6_
  19.6 0.2 late_square.1.refs_8_
  19.9 1.5 %collective-permute-start.9 = (bf16[2,128,128]{2,1,0:T(8,128)(2,1)S(1)}, bf16[2,128,128]{2,1,0:T(8,128)(2,1)S(1)}, u32[]{:S(2)}, u32[]{:S(2)}) collective-permute-start(bf16[2,128,128]{2,1,0:T(8,128)(2,1)S(1)} %late_square.1.refs_8_), channel_id=1, source_target_pairs={{0,2},{1,3},{2,0},{3,1},{4,6},{5,7},{6,4},{7,5},{8,10},{9,11},{10,... | collective-permute-start | bytes 196616 | tf_op jit(solution)/shard_map/ppermute | solution.py:21
  21.4 0.0 collective-permute-start.8
  21.4 2.8 %collective-permute-done.9.refs_2_ = bf16[2,128,128]{2,1,0:T(8,128)(2,1)S(1)} collective-permute-done((bf16[2,128,128]{2,1,0:T(8,128)(2,1)S(1)}, bf16[2,128,128]{2,1,0:T(8,128)(2,1)S(1)}, u32[]{:S(2)}, u32[]{:S(2)}) %collective-permute-start.9) | collective-permute-done | bytes 65568 | tf_op jit(solution)/shard_map/ppermute | solution.py:21
  24.2 0.0 collective-permute-start.10
  24.2 0.0 collective-permute-done.8.refs_9_
  24.2 0.8 %early_cube.1 = (bf16[2,128,128]{2,1,0:T(8,128)(2,1)}, f32[2,128,128]{2,1,0:T(8,128)S(1)}, bf16[5,128,256]{2,1,0:T(8,128)(2,1)S(1)}) custom-call(s32[72]{0:T(128)S(1)} %plan.1.refs_0_, bf16[2,128,128]{2,1,0:T(8,128)(2,1)S(1)} %join.3.refs_0_.refs_1_, bf16[2,128,128]{2,1,0:T(8,128)(2,1)S(1)} %collective-permute-done.refs_1_.refs_2_, ...), custom_call_target="tpu_custom_call" | custom-call | tf_op jit(solution)/shard_map/early_cube/pallas_call | solution.py:299
  25.0 0.4 %collective-permute-done.10.refs_3_ = bf16[2,128,128]{2,1,0:T(8,128)(2,1)S(1)} collective-permute-done((bf16[2,128,128]{2,1,0:T(8,128)(2,1)S(1)}, bf16[2,128,128]{2,1,0:T(8,128)(2,1)S(1)}, u32[]{:S(2)}, u32[]{:S(2)}) %collective-permute-start.10) | collective-permute-done | bytes 65568 | tf_op jit(solution)/shard_map/ppermute | solution.py:21
  25.5 0.9 %late_cube.1 = f32[2,128,128]{2,1,0:T(8,128)} custom-call(f32[2,128,128]{2,1,0:T(8,128)S(1)} %get-tuple-element.10.refs_0_, bf16[5,128,256]{2,1,0:T(8,128)(2,1)S(1)} %get-tuple-element.11.refs_1_, bf16[2,128,128]{2,1,0:T(8,128)(2,1)S(1)} %collective-permute-done.9.refs_2_, bf16[2,128,128]{2,1,0:T(8,128)(2,1)S(1)} %collective-permute-done.10.refs_3_), custom_call_target="tpu_custom_call" | custom-call | tf_op jit(solution)/shard_map/late_cube/pallas_call | solution.py:314
  (2 shorter events, 0.0 us)
Async XLA Ops:
  0.6 6.1 %collective-permute-start.6 = (bf16[2,128,128]{2,1,0:T(8,128)(2,1)}, bf16[2,128,128]{2,1,0:T(8,128)(2,1)S(1)}, u32[]{:S(2)}, u32[]{:S(2)}) collective-permute-start(bf16[2,128,128]{2,1,0:T(8,128)(2,1)} %bitcast.1.refs_0_), channel_id=1, source_target_pairs={{0,1},{1,0},{2,3},{3,2},{4,5},{5,4},{6,7},{7,6},{8,9},{9,8},{10,11... | collective-permute-start | bytes 196616 | tf_op jit(solution)/shard_map/ppermute | solution.py:21
  1.2 7.9 %collective-permute-start = (bf16[2,128,128]{2,1,0:T(8,128)(2,1)}, bf16[2,128,128]{2,1,0:T(8,128)(2,1)S(1)}, u32[]{:S(2)}, u32[]{:S(2)}) collective-permute-start(bf16[2,128,128]{2,1,0:T(8,128)(2,1)} %bitcast.1.refs_0_), channel_id=1, source_target_pairs={{0,24},{4,28},{8,16},{12,20},{16,8},{20,12},{24,0},{28,4},{1,25},{... | collective-permute-start | bytes 196616 | tf_op jit(solution)/shard_map/ppermute | solution.py:21
  5.9 4.5 %collective-permute-start.1 = (bf16[2,128,128]{2,1,0:T(8,128)(2,1)}, bf16[2,128,128]{2,1,0:T(8,128)(2,1)S(1)}, u32[]{:S(2)}, u32[]{:S(2)}) collective-permute-start(bf16[2,128,128]{2,1,0:T(8,128)(2,1)} %bitcast.1.refs_0_), channel_id=1, source_target_pairs={{0,8},{4,12},{8,0},{12,4},{16,24},{20,28},{24,16},{28,20},{1,9},{5... | collective-permute-start | bytes 196616 | tf_op jit(solution)/shard_map/ppermute | solution.py:21
  6.8 12.0 %collective-permute-start.7 = (bf16[4,128,128]{2,1,0:T(8,128)(2,1)S(1)}, bf16[4,128,128]{2,1,0:T(8,128)(2,1)S(1)}, u32[]{:S(2)}, u32[]{:S(2)}) collective-permute-start(bf16[4,128,128]{2,1,0:T(8,128)(2,1)S(1)} %join.5), channel_id=1, source_target_pairs={{0,2},{1,3},{2,0},{3,1},{4,6},{5,7},{6,4},{7,5},{8,10},{9,11},{10,... | collective-permute-start | bytes 393224 | tf_op jit(solution)/shard_map/ppermute | solution.py:21
  10.3 6.1 %copy-start = (s32[8,4,2]{0,2,1:T(2,128)S(1)}, s32[8,4,2]{0,2,1:T(2,128)}, u32[]{:S(2)}) copy-start(s32[8,4,2]{0,2,1:T(2,128)} %param.3) | copy-start | bytes 772
  10.4 9.3 %collective-permute-start.4 = (bf16[4,128,128]{2,1,0:T(8,128)(2,1)S(1)}, bf16[4,128,128]{2,1,0:T(8,128)(2,1)S(1)}, u32[]{:S(2)}, u32[]{:S(2)}) collective-permute-start(bf16[4,128,128]{2,1,0:T(8,128)(2,1)S(1)} %join.4), channel_id=1, source_target_pairs={{0,4},{4,0},{8,12},{12,8},{16,20},{20,16},{24,28},{28,24},{1,5},{5... | collective-permute-start | bytes 393224 | tf_op jit(solution)/shard_map/ppermute | solution.py:21
  12.0 5.9 %collective-permute-start.2 = (bf16[2,128,128]{2,1,0:T(8,128)(2,1)}, bf16[2,128,128]{2,1,0:T(8,128)(2,1)S(1)}, u32[]{:S(2)}, u32[]{:S(2)}) collective-permute-start(bf16[2,128,128]{2,1,0:T(8,128)(2,1)} %bitcast.1.refs_0_), channel_id=1, source_target_pairs={{0,4},{4,0},{8,12},{12,8},{16,20},{20,16},{24,28},{28,24},{1,5},{5... | collective-permute-start | bytes 196616 | tf_op jit(solution)/shard_map/ppermute | solution.py:21
  12.4 6.4 %collective-permute-start.3 = (bf16[2,128,128]{2,1,0:T(8,128)(2,1)}, bf16[2,128,128]{2,1,0:T(8,128)(2,1)S(1)}, u32[]{:S(2)}, u32[]{:S(2)}) collective-permute-start(bf16[2,128,128]{2,1,0:T(8,128)(2,1)} %bitcast.1.refs_0_), channel_id=1, source_target_pairs={{0,20},{4,16},{8,28},{12,24},{16,4},{20,0},{24,12},{28,8},{1,21},{... | collective-permute-start | bytes 196616 | tf_op jit(solution)/shard_map/ppermute | solution.py:21
  13.8 5.9 %collective-permute-start.5 = (bf16[2,128,128]{2,1,0:T(8,128)(2,1)S(1)}, bf16[2,128,128]{2,1,0:T(8,128)(2,1)S(1)}, u32[]{:S(2)}, u32[]{:S(2)}) collective-permute-start(bf16[2,128,128]{2,1,0:T(8,128)(2,1)S(1)} %collective-permute-done.refs_1_.refs_2_), channel_id=1, source_target_pairs={{0,8},{4,12},{8,0},{12,4},{16,24},{20,28},{24,16},{28,20},{1,9},{5... | collective-permute-start | bytes 196616 | tf_op jit(solution)/shard_map/ppermute | solution.py:21
  19.9 4.3 %collective-permute-start.9 = (bf16[2,128,128]{2,1,0:T(8,128)(2,1)S(1)}, bf16[2,128,128]{2,1,0:T(8,128)(2,1)S(1)}, u32[]{:S(2)}, u32[]{:S(2)}) collective-permute-start(bf16[2,128,128]{2,1,0:T(8,128)(2,1)S(1)} %late_square.1.refs_8_), channel_id=1, source_target_pairs={{0,2},{1,3},{2,0},{3,1},{4,6},{5,7},{6,4},{7,5},{8,10},{9,11},{10,... | collective-permute-start | bytes 196616 | tf_op jit(solution)/shard_map/ppermute | solution.py:21
  21.4 2.9 %collective-permute-start.8 = (bf16[2,128,128]{2,1,0:T(8,128)(2,1)S(1)}, bf16[2,128,128]{2,1,0:T(8,128)(2,1)S(1)}, u32[]{:S(2)}, u32[]{:S(2)}) collective-permute-start(bf16[2,128,128]{2,1,0:T(8,128)(2,1)S(1)} %late_square.1.refs_8_), channel_id=1, source_target_pairs={{0,1},{1,0},{2,3},{3,2},{4,5},{5,4},{6,7},{7,6},{8,9},{9,8},{10,11... | collective-permute-start | bytes 196616 | tf_op jit(solution)/shard_map/ppermute | solution.py:21
  24.2 1.3 %collective-permute-start.10 = (bf16[2,128,128]{2,1,0:T(8,128)(2,1)S(1)}, bf16[2,128,128]{2,1,0:T(8,128)(2,1)S(1)}, u32[]{:S(2)}, u32[]{:S(2)}) collective-permute-start(bf16[2,128,128]{2,1,0:T(8,128)(2,1)S(1)} %collective-permute-done.9.refs_2_), channel_id=1, source_target_pairs={{0,1},{1,0},{2,3},{3,2},{4,5},{5,4},{6,7},{7,6},{8,9},{9,8},{10,11... | collective-permute-start | bytes 196616 | tf_op jit(solution)/shard_map/ppermute | solution.py:21

commit v3 on v2

--- a/solution.py
+++ b/solution.py
@@ -46,29 +46,31 @@
 
 def column_order(row_count):
     far = far_rows(row_count)
-    early = [0] + [g + 2 for g in far] + [2, 1] + [g + 1 for g in far]
-    late = [3, far[0] + 3, far[0]]
+    early = [0] + [g + 2 for g in far] + [1, 2]
+    late = [3, far[0], far[0] + 3]
     for g in far[1:]:
-        late += [g + 3, g]
-    return early, late
+        late += [g, g + 3]
+    return early, late + [g + 1 for g in far]
 
 
 def gather(values, row_count, col_count):
     far = far_rows(row_count)
-    rows = {k: send(values, "row", k) for k in [g + 2 for g in far] + [2]}
+    rows = {k: send(values, "row", k) for k in [g + 2 for g in far] + [1]}
     near = send(values, "col", 1)
-    for k in [1] + [g + 1 for g in far]:
-        rows[k] = send(values, "row", k)
+    rows[2] = send(values, "row", 2)
     direct = list(rows.values())
+    slow = [send(values, "row", g + 1) for g in far]
     own = join(values)
-    pair = join(own, near)
-    lefts = [near] + [send(pair, "col", k) for k in range(2, col_count, 2)]
+    lefts = [near]
+    for k in range(2, col_count, 2):
+        lefts.append(send(values, "col", k))
+        lefts.append(send(lefts[-1], "col", 1))
     late = []
     for g in far:
         source = rows[g + 2]
-        late.append(send(source if late else join(rows[2], source), "row", 1))
-        late.append(send(source, "row", 2))
-    return own, direct, late, lefts
+        late.append(send(source if late else join(rows[1], source), "row", 2))
+        late.append(send(source, "row", 1))
+    return own, direct, late + slow, lefts
 
 
 def split(number, divisor):

time: 26.5 us -> 26.7 us (level)
  waiting for transfers between devices: 6.13 us -> 7.52 us
  starting transfers between devices: 14.4 us -> 13.4 us
  Pallas kernels: 5.12 us -> 4.26 us
  local copies, waits for them, and re-layouts: 0.01 us -> 0.68 us
    ppermute x11 -> x12, waiting for transfers between devices: 6.13 us -> 7.52 us  [send(): return lax.ppermute(array, axis, [(i, i ^ offset) for i in range(size)])]
    ppermute x11 -> x12, starting transfers between devices: 14.4 us -> 13.4 us  [send(): return lax.ppermute(array, axis, [(i, i ^ offset) for i in range(size)])]
    pallas_call x3 -> x2, Pallas kernels: 0.93 us -> 0.01 us  [join(): pl.pallas_call(join_kernel, out_shape=jax.ShapeDtypeStruct(shape, arrays[...]
    unnamed x2 -> x4, local copies, waits for them, and re-layouts: 0.01 us -> 0.68 us
  transfers between devices with their start and end apart: 11 -> 12, of which waited for: 5 -> 6; matrix products, arithmetic and copies ran while one was open for 0% -> 0% of each run, Pallas kernels for 15% -> 12%
where the time goes in v3:
time: 26.7 us; the launch traced here: 26.5 us
  starting transfers between devices  13.4 us (50%)
  waiting for transfers between devices  7.52 us (28%)
  Pallas kernels  4.26 us (16%)
  between operations  0.7 us (3%)
  local copies, waits for them, and re-layouts  0.68 us (3%)
    ppermute x12, starting transfers between devices, send(): return lax.ppermute(array, axis, [(i, i ^ offset) for i in range(size)])  13.4 us
    ppermute x12, waiting for transfers between devices, send(): return lax.ppermute(array, axis, [(i, i ^ offset) for i in range(size)])  7.52 us
    pallas_call x1, Pallas kernels, per_device(): pl.pallas_call(functools.partial(plan_kernel, sizes), out_shape=jax.Shape...  1.5 us
    pallas_call x1, Pallas kernels, per_device(): pl.pallas_call(functools.partial(late_cube_kernel, sizes, factor), out_sh...  0.86 us
    pallas_call x1, Pallas kernels, per_device(): pl.pallas_call(functools.partial(early_cube_kernel, sizes, factor, len(ri...  0.81 us
    pallas_call x1, Pallas kernels, per_device(): pl.pallas_call(functools.partial(early_square_kernel, sizes, len(early_ri...  0.78 us
    unnamed x4, local copies, waits for them, and re-layouts  0.68 us
  transfers between devices with their start and end apart: 12, of which 6 were waited for; matrix products, arithmetic and copies ran while one was open for 0% of the time, Pallas kernels for 12%

profile of v3, /device:TPU:0, one launch (start us, length us, event | category | flops | bytes accessed | tf_op | source)
XLA Modules:
  0.0 26.5 jit_solution(10382359398620767365)
XLA Ops:
  0.6 0.0 copy-start
  0.6 5.1 %collective-permute-start = (bf16[2,128,128]{2,1,0:T(8,128)(2,1)}, bf16[2,128,128]{2,1,0:T(8,128)(2,1)S(1)}, u32[]{:S(2)}, u32[]{:S(2)}) collective-permute-start(bf16[2,128,128]{2,1,0:T(8,128)(2,1)} %bitcast.4), channel_id=1, source_target_pairs={{0,24},{4,28},{8,16},{12,20},{16,8},{20,12},{24,0},{28,4},{1,25},{... | collective-permute-start | bytes 196616 | tf_op jit(solution)/shard_map/ppermute | solution.py:21
  5.8 1.5 %collective-permute-start.1 = (bf16[2,128,128]{2,1,0:T(8,128)(2,1)}, bf16[2,128,128]{2,1,0:T(8,128)(2,1)S(1)}, u32[]{:S(2)}, u32[]{:S(2)}) collective-permute-start(bf16[2,128,128]{2,1,0:T(8,128)(2,1)} %bitcast.5), channel_id=1, source_target_pairs={{0,4},{4,0},{8,12},{12,8},{16,20},{20,16},{24,28},{28,24},{1,5},{5... | collective-permute-start | bytes 196616 | tf_op jit(solution)/shard_map/ppermute | solution.py:21
  7.3 1.5 %collective-permute-start.7 = (bf16[2,128,128]{2,1,0:T(8,128)(2,1)}, bf16[2,128,128]{2,1,0:T(8,128)(2,1)S(1)}, u32[]{:S(2)}, u32[]{:S(2)}) collective-permute-start(bf16[2,128,128]{2,1,0:T(8,128)(2,1)} %bitcast.6), channel_id=1, source_target_pairs={{0,2},{1,3},{2,0},{3,1},{4,6},{5,7},{6,4},{7,5},{8,10},{9,11},{10,... | collective-permute-start | bytes 196616 | tf_op jit(solution)/shard_map/ppermute | solution.py:21
  8.8 0.0 collective-permute-start.2
  8.8 0.0 collective-permute-done.refs_1_.refs_2_
  8.8 1.5 %collective-permute-done.1.refs_0_.refs_3_ = bf16[2,128,128]{2,1,0:T(8,128)(2,1)S(1)} collective-permute-done((bf16[2,128,128]{2,1,0:T(8,128)(2,1)}, bf16[2,128,128]{2,1,0:T(8,128)(2,1)S(1)}, u32[]{:S(2)}, u32[]{:S(2)}) %collective-permute-start.1) | collective-permute-done | bytes 65568 | tf_op jit(solution)/shard_map/ppermute | solution.py:21
  10.3 0.6 %collective-permute-start.3 = (bf16[4,128,128]{2,1,0:T(8,128)(2,1)S(1)}, bf16[4,128,128]{2,1,0:T(8,128)(2,1)S(1)}, u32[]{:S(2)}, u32[]{:S(2)}) collective-permute-start(bf16[4,128,128]{2,1,0:T(8,128)(2,1)S(1)} %join.3), channel_id=1, source_target_pairs={{0,8},{4,12},{8,0},{12,4},{16,24},{20,28},{24,16},{28,20},{1,9},{5... | collective-permute-start | bytes 393224 | tf_op jit(solution)/shard_map/ppermute | solution.py:21
  10.9 0.0 copy-done
  10.9 0.0 collective-permute-start.6
  10.9 0.8 %collective-permute-done.7.refs_6_ = bf16[2,128,128]{2,1,0:T(8,128)(2,1)S(1)} collective-permute-done((bf16[2,128,128]{2,1,0:T(8,128)(2,1)}, bf16[2,128,128]{2,1,0:T(8,128)(2,1)S(1)}, u32[]{:S(2)}, u32[]{:S(2)}) %collective-permute-start.7) | collective-permute-done | bytes 65568 | tf_op jit(solution)/shard_map/ppermute | solution.py:21
  11.8 0.0 collective-permute-start.8
  11.8 2.7 %collective-permute-start.5 = (bf16[2,128,128]{2,1,0:T(8,128)(2,1)S(1)}, bf16[2,128,128]{2,1,0:T(8,128)(2,1)S(1)}, u32[]{:S(2)}, u32[]{:S(2)}) collective-permute-start(bf16[2,128,128]{2,1,0:T(8,128)(2,1)S(1)} %bitcast.9), channel_id=1, source_target_pairs={{0,20},{4,16},{8,28},{12,24},{16,4},{20,0},{24,12},{28,8},{1,21},{... | collective-permute-start | bytes 196616 | tf_op jit(solution)/shard_map/ppermute | solution.py:21
  14.5 0.0 collective-permute-done.2.refs_4_
  14.5 0.3 %collective-permute-start.4 = (bf16[2,128,128]{2,1,0:T(8,128)(2,1)S(1)}, bf16[2,128,128]{2,1,0:T(8,128)(2,1)S(1)}, u32[]{:S(2)}, u32[]{:S(2)}) collective-permute-start(bf16[2,128,128]{2,1,0:T(8,128)(2,1)S(1)} %collective-permute-done.refs_1_.refs_2_), channel_id=1, source_target_pairs={{0,4},{4,0},{8,12},{12,8},{16,20},{20,16},{24,28},{28,24},{1,5},{5... | collective-permute-start | bytes 196616 | tf_op jit(solution)/shard_map/ppermute | solution.py:21
  14.8 0.7 %copy-done.1 = s32[8,4,2]{0,2,1:T(2,128)S(1)} copy-done((s32[8,4,2]{0,2,1:T(2,128)S(1)}, s32[8,4,2]{0,2,1:T(2,128)}, u32[]{:S(2)}) %copy-start.1) | copy-done | bytes 280
  15.5 1.5 %plan.1.refs_0_ = s32[72]{0:T(128)S(1)} custom-call(s32[4,2,8]{2,1,0:T(2,128)S(1)} %bitcast.11), custom_call_target="tpu_custom_call" | custom-call | tf_op jit(solution)/shard_map/plan/pallas_call | solution.py:264
  17.0 0.0 collective-permute-done.6.refs_5_
  17.0 0.0 collective-permute-done.8.refs_7_
  17.0 0.8 %early_square.1 = (f32[2,128,128]{2,1,0:T(8,128)S(1)}, bf16[9,256,128]{2,1,0:T(8,128)(2,1)S(1)}) custom-call(s32[72]{0:T(128)S(1)} %plan.1.refs_0_, bf16[2,128,128]{2,1,0:T(8,128)(2,1)S(1)} %join.2.refs_1_, bf16[2,128,128]{2,1,0:T(8,128)(2,1)S(1)} %collective-permute-done.refs_1_.refs_2_, bf16[2,128,128]{2,1,0:T(8,128)(2,1)S(1)} %collective-permute-done.1.refs_0_.refs_3_, ...), custom_call_target="tpu_custom_call" | custom-call | tf_op jit(solution)/shard_map/early_square/pallas_call | solution.py:272
  17.8 1.8 %collective-permute-done.5.refs_4_.refs_7_ = bf16[2,128,128]{2,1,0:T(8,128)(2,1)S(1)} collective-permute-done((bf16[2,128,128]{2,1,0:T(8,128)(2,1)S(1)}, bf16[2,128,128]{2,1,0:T(8,128)(2,1)S(1)}, u32[]{:S(2)}, u32[]{:S(2)}) %collective-permute-start.5) | collective-permute-done | bytes 65568 | tf_op jit(solution)/shard_map/ppermute | solution.py:21
  19.6 0.2 collective-permute-done.4.refs_3_.refs_6_
  19.8 0.0 collective-permute-done.3.refs_2_.refs_5_
  19.8 0.3 %late_square.1.refs_8_ = bf16[2,128,128]{2,1,0:T(8,128)(2,1)S(1)} custom-call(f32[2,128,128]{2,1,0:T(8,128)S(1)} %get-tuple-element.7.refs_0_, bf16[9,256,128]{2,1,0:T(8,128)(2,1)S(1)} %get-tuple-element.8.refs_1_, bf16[4,128,128]{2,1,0:T(8,128)(2,1)S(1)} %collective-permute-done.3.refs_2_.refs_5_, ...), custom_call_target="tpu_custom_call" | custom-call | tf_op jit(solution)/shard_map/late_square/pallas_call | solution.py:286
  20.1 1.6 %collective-permute-start.10 = (bf16[2,128,128]{2,1,0:T(8,128)(2,1)S(1)}, bf16[2,128,128]{2,1,0:T(8,128)(2,1)S(1)}, u32[]{:S(2)}, u32[]{:S(2)}) collective-permute-start(bf16[2,128,128]{2,1,0:T(8,128)(2,1)S(1)} %late_square.1.refs_8_), channel_id=1, source_target_pairs={{0,2},{1,3},{2,0},{3,1},{4,6},{5,7},{6,4},{7,5},{8,10},{9,11},{10,... | collective-permute-start | bytes 196616 | tf_op jit(solution)/shard_map/ppermute | solution.py:21
  21.6 0.0 collective-permute-start.9
  21.6 2.8 %collective-permute-done.10.refs_2_ = bf16[2,128,128]{2,1,0:T(8,128)(2,1)S(1)} collective-permute-done((bf16[2,128,128]{2,1,0:T(8,128)(2,1)S(1)}, bf16[2,128,128]{2,1,0:T(8,128)(2,1)S(1)}, u32[]{:S(2)}, u32[]{:S(2)}) %collective-permute-start.10) | collective-permute-done | bytes 65568 | tf_op jit(solution)/shard_map/ppermute | solution.py:21
  24.4 0.0 collective-permute-start.11
  24.4 0.0 collective-permute-done.9.refs_9_
  24.4 0.8 %early_cube.1 = (bf16[2,128,128]{2,1,0:T(8,128)(2,1)}, f32[2,128,128]{2,1,0:T(8,128)S(1)}, bf16[5,128,256]{2,1,0:T(8,128)(2,1)S(1)}) custom-call(s32[72]{0:T(128)S(1)} %plan.1.refs_0_, bf16[2,128,128]{2,1,0:T(8,128)(2,1)S(1)} %join.2.refs_1_, bf16[2,128,128]{2,1,0:T(8,128)(2,1)S(1)} %collective-permute-done.refs_1_.refs_2_, ...), custom_call_target="tpu_custom_call" | custom-call | tf_op jit(solution)/shard_map/early_cube/pallas_call | solution.py:301
  25.2 0.4 %collective-permute-done.11.refs_3_ = bf16[2,128,128]{2,1,0:T(8,128)(2,1)S(1)} collective-permute-done((bf16[2,128,128]{2,1,0:T(8,128)(2,1)S(1)}, bf16[2,128,128]{2,1,0:T(8,128)(2,1)S(1)}, u32[]{:S(2)}, u32[]{:S(2)}) %collective-permute-start.11) | collective-permute-done | bytes 65568 | tf_op jit(solution)/shard_map/ppermute | solution.py:21
  25.7 0.9 %late_cube.1 = f32[2,128,128]{2,1,0:T(8,128)} custom-call(f32[2,128,128]{2,1,0:T(8,128)S(1)} %get-tuple-element.10.refs_0_, bf16[5,128,256]{2,1,0:T(8,128)(2,1)S(1)} %get-tuple-element.11.refs_1_, bf16[2,128,128]{2,1,0:T(8,128)(2,1)S(1)} %collective-permute-done.10.refs_2_, bf16[2,128,128]{2,1,0:T(8,128)(2,1)S(1)} %collective-permute-done.11.refs_3_), custom_call_target="tpu_custom_call" | custom-call | tf_op jit(solution)/shard_map/late_cube/pallas_call | solution.py:316
  (3 shorter events, 0.0 us)
Async XLA Ops:
  0.6 10.3 %copy-start = (bf16[1,1,2,128,128]{4,3,2,1,0:T(8,128)(2,1)S(1)}, bf16[1,1,2,128,128]{4,3,2,1,0:T(8,128)(2,1)}, u32[]{:S(2)}) copy-start(bf16[1,1,2,128,128]{4,3,2,1,0:T(8,128)(2,1)} %param.2) | copy-start | bytes 196612
  0.6 8.2 %collective-permute-start = (bf16[2,128,128]{2,1,0:T(8,128)(2,1)}, bf16[2,128,128]{2,1,0:T(8,128)(2,1)S(1)}, u32[]{:S(2)}, u32[]{:S(2)}) collective-permute-start(bf16[2,128,128]{2,1,0:T(8,128)(2,1)} %bitcast.4), channel_id=1, source_target_pairs={{0,24},{4,28},{8,16},{12,20},{16,8},{20,12},{24,0},{28,4},{1,25},{... | collective-permute-start | bytes 196616 | tf_op jit(solution)/shard_map/ppermute | solution.py:21
  5.8 4.5 %collective-permute-start.1 = (bf16[2,128,128]{2,1,0:T(8,128)(2,1)}, bf16[2,128,128]{2,1,0:T(8,128)(2,1)S(1)}, u32[]{:S(2)}, u32[]{:S(2)}) collective-permute-start(bf16[2,128,128]{2,1,0:T(8,128)(2,1)} %bitcast.5), channel_id=1, source_target_pairs={{0,4},{4,0},{8,12},{12,8},{16,20},{20,16},{24,28},{28,24},{1,5},{5... | collective-permute-start | bytes 196616 | tf_op jit(solution)/shard_map/ppermute | solution.py:21
  7.3 4.5 %collective-permute-start.7 = (bf16[2,128,128]{2,1,0:T(8,128)(2,1)}, bf16[2,128,128]{2,1,0:T(8,128)(2,1)S(1)}, u32[]{:S(2)}, u32[]{:S(2)}) collective-permute-start(bf16[2,128,128]{2,1,0:T(8,128)(2,1)} %bitcast.6), channel_id=1, source_target_pairs={{0,2},{1,3},{2,0},{3,1},{4,6},{5,7},{6,4},{7,5},{8,10},{9,11},{10,... | collective-permute-start | bytes 196616 | tf_op jit(solution)/shard_map/ppermute | solution.py:21
  8.8 5.7 %collective-permute-start.2 = (bf16[2,128,128]{2,1,0:T(8,128)(2,1)}, bf16[2,128,128]{2,1,0:T(8,128)(2,1)S(1)}, u32[]{:S(2)}, u32[]{:S(2)}) collective-permute-start(bf16[2,128,128]{2,1,0:T(8,128)(2,1)} %bitcast.7), channel_id=1, source_target_pairs={{0,8},{4,12},{8,0},{12,4},{16,24},{20,28},{24,16},{28,20},{1,9},{5... | collective-permute-start | bytes 196616 | tf_op jit(solution)/shard_map/ppermute | solution.py:21
  10.3 9.5 %collective-permute-start.3 = (bf16[4,128,128]{2,1,0:T(8,128)(2,1)S(1)}, bf16[4,128,128]{2,1,0:T(8,128)(2,1)S(1)}, u32[]{:S(2)}, u32[]{:S(2)}) collective-permute-start(bf16[4,128,128]{2,1,0:T(8,128)(2,1)S(1)} %join.3), channel_id=1, source_target_pairs={{0,8},{4,12},{8,0},{12,4},{16,24},{20,28},{24,16},{28,20},{1,9},{5... | collective-permute-start | bytes 393224 | tf_op jit(solution)/shard_map/ppermute | solution.py:21
  10.9 6.1 %collective-permute-start.6 = (bf16[2,128,128]{2,1,0:T(8,128)(2,1)S(1)}, bf16[2,128,128]{2,1,0:T(8,128)(2,1)S(1)}, u32[]{:S(2)}, u32[]{:S(2)}) collective-permute-start(bf16[2,128,128]{2,1,0:T(8,128)(2,1)S(1)} %bitcast.8), channel_id=1, source_target_pairs={{0,1},{1,0},{2,3},{3,2},{4,5},{5,4},{6,7},{7,6},{8,9},{9,8},{10,11... | collective-permute-start | bytes 196616 | tf_op jit(solution)/shard_map/ppermute | solution.py:21
  11.8 5.2 %collective-permute-start.8 = (bf16[2,128,128]{2,1,0:T(8,128)(2,1)S(1)}, bf16[2,128,128]{2,1,0:T(8,128)(2,1)S(1)}, u32[]{:S(2)}, u32[]{:S(2)}) collective-permute-start(bf16[2,128,128]{2,1,0:T(8,128)(2,1)S(1)} %collective-permute-done.7.refs_6_), channel_id=1, source_target_pairs={{0,1},{1,0},{2,3},{3,2},{4,5},{5,4},{6,7},{7,6},{8,9},{9,8},{10,11... | collective-permute-start | bytes 196616 | tf_op jit(solution)/shard_map/ppermute | solution.py:21
  11.8 7.8 %collective-permute-start.5 = (bf16[2,128,128]{2,1,0:T(8,128)(2,1)S(1)}, bf16[2,128,128]{2,1,0:T(8,128)(2,1)S(1)}, u32[]{:S(2)}, u32[]{:S(2)}) collective-permute-start(bf16[2,128,128]{2,1,0:T(8,128)(2,1)S(1)} %bitcast.9), channel_id=1, source_target_pairs={{0,20},{4,16},{8,28},{12,24},{16,4},{20,0},{24,12},{28,8},{1,21},{... | collective-permute-start | bytes 196616 | tf_op jit(solution)/shard_map/ppermute | solution.py:21
  14.5 5.3 %collective-permute-start.4 = (bf16[2,128,128]{2,1,0:T(8,128)(2,1)S(1)}, bf16[2,128,128]{2,1,0:T(8,128)(2,1)S(1)}, u32[]{:S(2)}, u32[]{:S(2)}) collective-permute-start(bf16[2,128,128]{2,1,0:T(8,128)(2,1)S(1)} %collective-permute-done.refs_1_.refs_2_), channel_id=1, source_target_pairs={{0,4},{4,0},{8,12},{12,8},{16,20},{20,16},{24,28},{28,24},{1,5},{5... | collective-permute-start | bytes 196616 | tf_op jit(solution)/shard_map/ppermute | solution.py:21
  14.8 0.7 %copy-start.1 = (s32[8,4,2]{0,2,1:T(2,128)S(1)}, s32[8,4,2]{0,2,1:T(2,128)}, u32[]{:S(2)}) copy-start(s32[8,4,2]{0,2,1:T(2,128)} %param.3) | copy-start | bytes 772
  20.1 4.3 %collective-permute-start.10 = (bf16[2,128,128]{2,1,0:T(8,128)(2,1)S(1)}, bf16[2,128,128]{2,1,0:T(8,128)(2,1)S(1)}, u32[]{:S(2)}, u32[]{:S(2)}) collective-permute-start(bf16[2,128,128]{2,1,0:T(8,128)(2,1)S(1)} %late_square.1.refs_8_), channel_id=1, source_target_pairs={{0,2},{1,3},{2,0},{3,1},{4,6},{5,7},{6,4},{7,5},{8,10},{9,11},{10,... | collective-permute-start | bytes 196616 | tf_op jit(solution)/shard_map/ppermute | solution.py:21
  21.6 2.8 %collective-permute-start.9 = (bf16[2,128,128]{2,1,0:T(8,128)(2,1)S(1)}, bf16[2,128,128]{2,1,0:T(8,128)(2,1)S(1)}, u32[]{:S(2)}, u32[]{:S(2)}) collective-permute-start(bf16[2,128,128]{2,1,0:T(8,128)(2,1)S(1)} %late_square.1.refs_8_), channel_id=1, source_target_pairs={{0,1},{1,0},{2,3},{3,2},{4,5},{5,4},{6,7},{7,6},{8,9},{9,8},{10,11... | collective-permute-start | bytes 196616 | tf_op jit(solution)/shard_map/ppermute | solution.py:21
  24.4 1.3 %collective-permute-start.11 = (bf16[2,128,128]{2,1,0:T(8,128)(2,1)S(1)}, bf16[2,128,128]{2,1,0:T(8,128)(2,1)S(1)}, u32[]{:S(2)}, u32[]{:S(2)}) collective-permute-start(bf16[2,128,128]{2,1,0:T(8,128)(2,1)S(1)} %collective-permute-done.10.refs_2_), channel_id=1, source_target_pairs={{0,1},{1,0},{2,3},{3,2},{4,5},{5,4},{6,7},{7,6},{8,9},{9,8},{10,11... | collective-permute-start | bytes 196616 | tf_op jit(solution)/shard_map/ppermute | solution.py:21

commit v4 on v3

--- a/solution.py
+++ b/solution.py
@@ -63,8 +63,8 @@
     own = join(values)
     lefts = [near]
     for k in range(2, col_count, 2):
-        lefts.append(send(values, "col", k))
-        lefts.append(send(lefts[-1], "col", 1))
+        cross = send(values, "col", k + 1)
+        lefts += [send(cross, "col", 1), cross]
     late = []
     for g in far:
         source = rows[g + 2]
@@ -293,10 +293,10 @@
     )(partial, factors, *forwarded)
 
     far = range(2, col_count, 2)
-    others = {k: send(square, "col", k) for k in far}
+    others = {k + 1: send(square, "col", k + 1) for k in far}
     others[1] = send(square, "col", 1)
     for k in far:
-        others[k + 1] = send(others[k], "col", 1)
+        others[k] = send(others[k + 1], "col", 1)
     rights = early_rights + forwarded
     square_out, partial, factors = pl.pallas_call(
         functools.partial(early_cube_kernel, sizes, factor, len(rights)),

time: 26.7 us -> 26.5 us (level)
  starting transfers between devices: 13.4 us -> 11.7 us
  waiting for transfers between devices: 7.52 us -> 8.98 us
    ppermute x12, starting transfers between devices: 13.4 us -> 11.7 us  [send(): return lax.ppermute(array, axis, [(i, i ^ offset) for i in range(size)])]
    ppermute x12, waiting for transfers between devices: 7.52 us -> 8.98 us  [send(): return lax.ppermute(array, axis, [(i, i ^ offset) for i in range(size)])]
where the time goes in v4:
time: 26.5 us; the launch traced here: 26.3 us
  starting transfers between devices  11.7 us (44%)
  waiting for transfers between devices  8.98 us (34%)
  Pallas kernels  4.25 us (16%)
  between operations  0.71 us (3%)
  local copies, waits for them, and re-layouts  0.68 us (3%)
    ppermute x12, starting transfers between devices, send(): return lax.ppermute(array, axis, [(i, i ^ offset) for i in range(size)])  11.7 us
    ppermute x12, waiting for transfers between devices, send(): return lax.ppermute(array, axis, [(i, i ^ offset) for i in range(size)])  8.98 us
    pallas_call x1, Pallas kernels, per_device(): pl.pallas_call(functools.partial(plan_kernel, sizes), out_shape=jax.Shape...  1.5 us
    pallas_call x1, Pallas kernels, per_device(): pl.pallas_call(functools.partial(late_cube_kernel, sizes, factor), out_sh...  0.86 us
    pallas_call x1, Pallas kernels, per_device(): pl.pallas_call(functools.partial(early_cube_kernel, sizes, factor, len(ri...  0.81 us
    pallas_call x1, Pallas kernels, per_device(): pl.pallas_call(functools.partial(early_square_kernel, sizes, len(early_ri...  0.78 us
    unnamed x4, local copies, waits for them, and re-layouts  0.68 us
  transfers between devices with their start and end apart: 12, of which 6 were waited for; matrix products, arithmetic and copies ran while one was open for 0% of the time, Pallas kernels for 12%

profile of v4, /device:TPU:0, one launch (start us, length us, event | category | flops | bytes accessed | tf_op | source)
XLA Modules:
  0.0 26.3 jit_solution(12676306227123107295)
XLA Ops:
  0.6 0.0 copy-start
  0.6 5.1 %collective-permute-start = (bf16[2,128,128]{2,1,0:T(8,128)(2,1)}, bf16[2,128,128]{2,1,0:T(8,128)(2,1)S(1)}, u32[]{:S(2)}, u32[]{:S(2)}) collective-permute-start(bf16[2,128,128]{2,1,0:T(8,128)(2,1)} %bitcast.4), channel_id=1, source_target_pairs={{0,24},{4,28},{8,16},{12,20},{16,8},{20,12},{24,0},{28,4},{1,25},{... | collective-permute-start | bytes 196616 | tf_op jit(solution)/shard_map/ppermute | solution.py:21
  5.8 1.5 %collective-permute-start.1 = (bf16[2,128,128]{2,1,0:T(8,128)(2,1)}, bf16[2,128,128]{2,1,0:T(8,128)(2,1)S(1)}, u32[]{:S(2)}, u32[]{:S(2)}) collective-permute-start(bf16[2,128,128]{2,1,0:T(8,128)(2,1)} %bitcast.5), channel_id=1, source_target_pairs={{0,4},{4,0},{8,12},{12,8},{16,20},{20,16},{24,28},{28,24},{1,5},{5... | collective-permute-start | bytes 196616 | tf_op jit(solution)/shard_map/ppermute | solution.py:21
  7.3 0.4 %collective-permute-start.7 = (bf16[2,128,128]{2,1,0:T(8,128)(2,1)}, bf16[2,128,128]{2,1,0:T(8,128)(2,1)S(1)}, u32[]{:S(2)}, u32[]{:S(2)}) collective-permute-start(bf16[2,128,128]{2,1,0:T(8,128)(2,1)} %bitcast.6), channel_id=1, source_target_pairs={{0,3},{1,2},{2,1},{3,0},{4,7},{5,6},{6,5},{7,4},{8,11},{9,10},{10,... | collective-permute-start | bytes 196616 | tf_op jit(solution)/shard_map/ppermute | solution.py:21
  7.7 0.0 collective-permute-start.2
  7.7 0.6 %collective-permute-done.refs_1_.refs_2_ = bf16[2,128,128]{2,1,0:T(8,128)(2,1)S(1)} collective-permute-done((bf16[2,128,128]{2,1,0:T(8,128)(2,1)}, bf16[2,128,128]{2,1,0:T(8,128)(2,1)S(1)}, u32[]{:S(2)}, u32[]{:S(2)}) %collective-permute-start) | collective-permute-done | bytes 65568 | tf_op jit(solution)/shard_map/ppermute | solution.py:21
  8.2 2.0 %collective-permute-done.1.refs_0_.refs_3_ = bf16[2,128,128]{2,1,0:T(8,128)(2,1)S(1)} collective-permute-done((bf16[2,128,128]{2,1,0:T(8,128)(2,1)}, bf16[2,128,128]{2,1,0:T(8,128)(2,1)S(1)}, u32[]{:S(2)}, u32[]{:S(2)}) %collective-permute-start.1) | collective-permute-done | bytes 65568 | tf_op jit(solution)/shard_map/ppermute | solution.py:21
  10.3 0.1 collective-permute-start.3
  10.4 0.0 copy-done
  10.4 0.1 collective-permute-start.6
  10.5 1.3 %collective-permute-done.7.refs_7_ = bf16[2,128,128]{2,1,0:T(8,128)(2,1)S(1)} collective-permute-done((bf16[2,128,128]{2,1,0:T(8,128)(2,1)}, bf16[2,128,128]{2,1,0:T(8,128)(2,1)S(1)}, u32[]{:S(2)}, u32[]{:S(2)}) %collective-permute-start.7) | collective-permute-done | bytes 65568 | tf_op jit(solution)/shard_map/ppermute | solution.py:21
  11.8 0.2 collective-permute-start.8
  12.0 2.2 %collective-permute-start.5 = (bf16[2,128,128]{2,1,0:T(8,128)(2,1)S(1)}, bf16[2,128,128]{2,1,0:T(8,128)(2,1)S(1)}, u32[]{:S(2)}, u32[]{:S(2)}) collective-permute-start(bf16[2,128,128]{2,1,0:T(8,128)(2,1)S(1)} %bitcast.9), channel_id=1, source_target_pairs={{0,20},{4,16},{8,28},{12,24},{16,4},{20,0},{24,12},{28,8},{1,21},{... | collective-permute-start | bytes 196616 | tf_op jit(solution)/shard_map/ppermute | solution.py:21
  14.1 0.0 collective-permute-done.2.refs_4_
  14.2 0.6 %collective-permute-start.4 = (bf16[2,128,128]{2,1,0:T(8,128)(2,1)S(1)}, bf16[2,128,128]{2,1,0:T(8,128)(2,1)S(1)}, u32[]{:S(2)}, u32[]{:S(2)}) collective-permute-start(bf16[2,128,128]{2,1,0:T(8,128)(2,1)S(1)} %collective-permute-done.refs_1_.refs_2_), channel_id=1, source_target_pairs={{0,4},{4,0},{8,12},{12,8},{16,20},{20,16},{24,28},{28,24},{1,5},{5... | collective-permute-start | bytes 196616 | tf_op jit(solution)/shard_map/ppermute | solution.py:21
  14.7 0.7 %copy-done.1 = s32[8,4,2]{0,2,1:T(2,128)S(1)} copy-done((s32[8,4,2]{0,2,1:T(2,128)S(1)}, s32[8,4,2]{0,2,1:T(2,128)}, u32[]{:S(2)}) %copy-start.1) | copy-done | bytes 280
  15.4 1.5 %plan.1.refs_0_ = s32[72]{0:T(128)S(1)} custom-call(s32[4,2,8]{2,1,0:T(2,128)S(1)} %bitcast.11), custom_call_target="tpu_custom_call" | custom-call | tf_op jit(solution)/shard_map/plan/pallas_call | solution.py:264
  16.9 0.0 collective-permute-done.6.refs_5_
  16.9 0.0 collective-permute-done.8.refs_6_
  16.9 0.8 %early_square.1 = (f32[2,128,128]{2,1,0:T(8,128)S(1)}, bf16[9,256,128]{2,1,0:T(8,128)(2,1)S(1)}) custom-call(s32[72]{0:T(128)S(1)} %plan.1.refs_0_, bf16[2,128,128]{2,1,0:T(8,128)(2,1)S(1)} %join.2.refs_1_, bf16[2,128,128]{2,1,0:T(8,128)(2,1)S(1)} %collective-permute-done.refs_1_.refs_2_, bf16[2,128,128]{2,1,0:T(8,128)(2,1)S(1)} %collective-permute-done.1.refs_0_.refs_3_, ...), custom_call_target="tpu_custom_call" | custom-call | tf_op jit(solution)/shard_map/early_square/pallas_call | solution.py:272
  17.7 1.8 %collective-permute-done.5.refs_4_.refs_7_ = bf16[2,128,128]{2,1,0:T(8,128)(2,1)S(1)} collective-permute-done((bf16[2,128,128]{2,1,0:T(8,128)(2,1)S(1)}, bf16[2,128,128]{2,1,0:T(8,128)(2,1)S(1)}, u32[]{:S(2)}, u32[]{:S(2)}) %collective-permute-start.5) | collective-permute-done | bytes 65568 | tf_op jit(solution)/shard_map/ppermute | solution.py:21
  19.5 0.0 collective-permute-done.4.refs_3_.refs_6_
  19.5 0.0 collective-permute-done.3.refs_2_.refs_5_
  19.5 0.3 %late_square.1.refs_8_ = bf16[2,128,128]{2,1,0:T(8,128)(2,1)S(1)} custom-call(f32[2,128,128]{2,1,0:T(8,128)S(1)} %get-tuple-element.7.refs_0_, bf16[9,256,128]{2,1,0:T(8,128)(2,1)S(1)} %get-tuple-element.8.refs_1_, bf16[4,128,128]{2,1,0:T(8,128)(2,1)S(1)} %collective-permute-done.3.refs_2_.refs_5_, ...), custom_call_target="tpu_custom_call" | custom-call | tf_op jit(solution)/shard_map/late_square/pallas_call | solution.py:286
  19.8 0.4 %collective-permute-start.10 = (bf16[2,128,128]{2,1,0:T(8,128)(2,1)S(1)}, bf16[2,128,128]{2,1,0:T(8,128)(2,1)S(1)}, u32[]{:S(2)}, u32[]{:S(2)}) collective-permute-start(bf16[2,128,128]{2,1,0:T(8,128)(2,1)S(1)} %late_square.1.refs_8_), channel_id=1, source_target_pairs={{0,3},{1,2},{2,1},{3,0},{4,7},{5,6},{6,5},{7,4},{8,11},{9,10},{10,... | collective-permute-start | bytes 196616 | tf_op jit(solution)/shard_map/ppermute | solution.py:21
  20.2 1.1 %collective-permute-start.9 = (bf16[2,128,128]{2,1,0:T(8,128)(2,1)S(1)}, bf16[2,128,128]{2,1,0:T(8,128)(2,1)S(1)}, u32[]{:S(2)}, u32[]{:S(2)}) collective-permute-start(bf16[2,128,128]{2,1,0:T(8,128)(2,1)S(1)} %late_square.1.refs_8_), channel_id=1, source_target_pairs={{0,1},{1,0},{2,3},{3,2},{4,5},{5,4},{6,7},{7,6},{8,9},{9,8},{10,11... | collective-permute-start | bytes 196616 | tf_op jit(solution)/shard_map/ppermute | solution.py:21
  21.3 2.9 %collective-permute-done.10.refs_3_ = bf16[2,128,128]{2,1,0:T(8,128)(2,1)S(1)} collective-permute-done((bf16[2,128,128]{2,1,0:T(8,128)(2,1)S(1)}, bf16[2,128,128]{2,1,0:T(8,128)(2,1)S(1)}, u32[]{:S(2)}, u32[]{:S(2)}) %collective-permute-start.10) | collective-permute-done | bytes 65568 | tf_op jit(solution)/shard_map/ppermute | solution.py:21
  24.2 0.1 collective-permute-start.11
  24.3 0.0 collective-permute-done.9.refs_9_
  24.3 0.8 %early_cube.1 = (bf16[2,128,128]{2,1,0:T(8,128)(2,1)}, f32[2,128,128]{2,1,0:T(8,128)S(1)}, bf16[5,128,256]{2,1,0:T(8,128)(2,1)S(1)}) custom-call(s32[72]{0:T(128)S(1)} %plan.1.refs_0_, bf16[2,128,128]{2,1,0:T(8,128)(2,1)S(1)} %join.2.refs_1_, bf16[2,128,128]{2,1,0:T(8,128)(2,1)S(1)} %collective-permute-done.refs_1_.refs_2_, ...), custom_call_target="tpu_custom_call" | custom-call | tf_op jit(solution)/shard_map/early_cube/pallas_call | solution.py:301
  25.2 0.3 %collective-permute-done.11.refs_2_ = bf16[2,128,128]{2,1,0:T(8,128)(2,1)S(1)} collective-permute-done((bf16[2,128,128]{2,1,0:T(8,128)(2,1)S(1)}, bf16[2,128,128]{2,1,0:T(8,128)(2,1)S(1)}, u32[]{:S(2)}, u32[]{:S(2)}) %collective-permute-start.11) | collective-permute-done | bytes 65568 | tf_op jit(solution)/shard_map/ppermute | solution.py:21
  25.5 0.9 %late_cube.1 = f32[2,128,128]{2,1,0:T(8,128)} custom-call(f32[2,128,128]{2,1,0:T(8,128)S(1)} %get-tuple-element.10.refs_0_, bf16[5,128,256]{2,1,0:T(8,128)(2,1)S(1)} %get-tuple-element.11.refs_1_, bf16[2,128,128]{2,1,0:T(8,128)(2,1)S(1)} %collective-permute-done.11.refs_2_, bf16[2,128,128]{2,1,0:T(8,128)(2,1)S(1)} %collective-permute-done.10.refs_3_), custom_call_target="tpu_custom_call" | custom-call | tf_op jit(solution)/shard_map/late_cube/pallas_call | solution.py:316
  (3 shorter events, 0.0 us)
Async XLA Ops:
  0.6 9.7 %copy-start = (bf16[1,1,2,128,128]{4,3,2,1,0:T(8,128)(2,1)S(1)}, bf16[1,1,2,128,128]{4,3,2,1,0:T(8,128)(2,1)}, u32[]{:S(2)}) copy-start(bf16[1,1,2,128,128]{4,3,2,1,0:T(8,128)(2,1)} %param.2) | copy-start | bytes 196612
  0.6 7.6 %collective-permute-start = (bf16[2,128,128]{2,1,0:T(8,128)(2,1)}, bf16[2,128,128]{2,1,0:T(8,128)(2,1)S(1)}, u32[]{:S(2)}, u32[]{:S(2)}) collective-permute-start(bf16[2,128,128]{2,1,0:T(8,128)(2,1)} %bitcast.4), channel_id=1, source_target_pairs={{0,24},{4,28},{8,16},{12,20},{16,8},{20,12},{24,0},{28,4},{1,25},{... | collective-permute-start | bytes 196616 | tf_op jit(solution)/shard_map/ppermute | solution.py:21
  5.8 4.5 %collective-permute-start.1 = (bf16[2,128,128]{2,1,0:T(8,128)(2,1)}, bf16[2,128,128]{2,1,0:T(8,128)(2,1)S(1)}, u32[]{:S(2)}, u32[]{:S(2)}) collective-permute-start(bf16[2,128,128]{2,1,0:T(8,128)(2,1)} %bitcast.5), channel_id=1, source_target_pairs={{0,4},{4,0},{8,12},{12,8},{16,20},{20,16},{24,28},{28,24},{1,5},{5... | collective-permute-start | bytes 196616 | tf_op jit(solution)/shard_map/ppermute | solution.py:21
  7.3 4.5 %collective-permute-start.7 = (bf16[2,128,128]{2,1,0:T(8,128)(2,1)}, bf16[2,128,128]{2,1,0:T(8,128)(2,1)S(1)}, u32[]{:S(2)}, u32[]{:S(2)}) collective-permute-start(bf16[2,128,128]{2,1,0:T(8,128)(2,1)} %bitcast.6), channel_id=1, source_target_pairs={{0,3},{1,2},{2,1},{3,0},{4,7},{5,6},{6,5},{7,4},{8,11},{9,10},{10,... | collective-permute-start | bytes 196616 | tf_op jit(solution)/shard_map/ppermute | solution.py:21
  7.7 6.5 %collective-permute-start.2 = (bf16[2,128,128]{2,1,0:T(8,128)(2,1)}, bf16[2,128,128]{2,1,0:T(8,128)(2,1)S(1)}, u32[]{:S(2)}, u32[]{:S(2)}) collective-permute-start(bf16[2,128,128]{2,1,0:T(8,128)(2,1)} %bitcast.7), channel_id=1, source_target_pairs={{0,8},{4,12},{8,0},{12,4},{16,24},{20,28},{24,16},{28,20},{1,9},{5... | collective-permute-start | bytes 196616 | tf_op jit(solution)/shard_map/ppermute | solution.py:21
  10.3 9.3 %collective-permute-start.3 = (bf16[4,128,128]{2,1,0:T(8,128)(2,1)S(1)}, bf16[4,128,128]{2,1,0:T(8,128)(2,1)S(1)}, u32[]{:S(2)}, u32[]{:S(2)}) collective-permute-start(bf16[4,128,128]{2,1,0:T(8,128)(2,1)S(1)} %join.3), channel_id=1, source_target_pairs={{0,8},{4,12},{8,0},{12,4},{16,24},{20,28},{24,16},{28,20},{1,9},{5... | collective-permute-start | bytes 393224 | tf_op jit(solution)/shard_map/ppermute | solution.py:21
  10.4 6.5 %collective-permute-start.6 = (bf16[2,128,128]{2,1,0:T(8,128)(2,1)S(1)}, bf16[2,128,128]{2,1,0:T(8,128)(2,1)S(1)}, u32[]{:S(2)}, u32[]{:S(2)}) collective-permute-start(bf16[2,128,128]{2,1,0:T(8,128)(2,1)S(1)} %bitcast.8), channel_id=1, source_target_pairs={{0,1},{1,0},{2,3},{3,2},{4,5},{5,4},{6,7},{7,6},{8,9},{9,8},{10,11... | collective-permute-start | bytes 196616 | tf_op jit(solution)/shard_map/ppermute | solution.py:21
  11.8 5.1 %collective-permute-start.8 = (bf16[2,128,128]{2,1,0:T(8,128)(2,1)S(1)}, bf16[2,128,128]{2,1,0:T(8,128)(2,1)S(1)}, u32[]{:S(2)}, u32[]{:S(2)}) collective-permute-start(bf16[2,128,128]{2,1,0:T(8,128)(2,1)S(1)} %collective-permute-done.7.refs_7_), channel_id=1, source_target_pairs={{0,1},{1,0},{2,3},{3,2},{4,5},{5,4},{6,7},{7,6},{8,9},{9,8},{10,11... | collective-permute-start | bytes 196616 | tf_op jit(solution)/shard_map/ppermute | solution.py:21
  12.0 7.5 %collective-permute-start.5 = (bf16[2,128,128]{2,1,0:T(8,128)(2,1)S(1)}, bf16[2,128,128]{2,1,0:T(8,128)(2,1)S(1)}, u32[]{:S(2)}, u32[]{:S(2)}) collective-permute-start(bf16[2,128,128]{2,1,0:T(8,128)(2,1)S(1)} %bitcast.9), channel_id=1, source_target_pairs={{0,20},{4,16},{8,28},{12,24},{16,4},{20,0},{24,12},{28,8},{1,21},{... | collective-permute-start | bytes 196616 | tf_op jit(solution)/shard_map/ppermute | solution.py:21
  14.2 5.4 %collective-permute-start.4 = (bf16[2,128,128]{2,1,0:T(8,128)(2,1)S(1)}, bf16[2,128,128]{2,1,0:T(8,128)(2,1)S(1)}, u32[]{:S(2)}, u32[]{:S(2)}) collective-permute-start(bf16[2,128,128]{2,1,0:T(8,128)(2,1)S(1)} %collective-permute-done.refs_1_.refs_2_), channel_id=1, source_target_pairs={{0,4},{4,0},{8,12},{12,8},{16,20},{20,16},{24,28},{28,24},{1,5},{5... | collective-permute-start | bytes 196616 | tf_op jit(solution)/shard_map/ppermute | solution.py:21
  14.7 0.7 %copy-start.1 = (s32[8,4,2]{0,2,1:T(2,128)S(1)}, s32[8,4,2]{0,2,1:T(2,128)}, u32[]{:S(2)}) copy-start(s32[8,4,2]{0,2,1:T(2,128)} %param.3) | copy-start | bytes 772
  19.8 4.4 %collective-permute-start.10 = (bf16[2,128,128]{2,1,0:T(8,128)(2,1)S(1)}, bf16[2,128,128]{2,1,0:T(8,128)(2,1)S(1)}, u32[]{:S(2)}, u32[]{:S(2)}) collective-permute-start(bf16[2,128,128]{2,1,0:T(8,128)(2,1)S(1)} %late_square.1.refs_8_), channel_id=1, source_target_pairs={{0,3},{1,2},{2,1},{3,0},{4,7},{5,6},{6,5},{7,4},{8,11},{9,10},{10,... | collective-permute-start | bytes 196616 | tf_op jit(solution)/shard_map/ppermute | solution.py:21
  20.2 4.2 %collective-permute-start.9 = (bf16[2,128,128]{2,1,0:T(8,128)(2,1)S(1)}, bf16[2,128,128]{2,1,0:T(8,128)(2,1)S(1)}, u32[]{:S(2)}, u32[]{:S(2)}) collective-permute-start(bf16[2,128,128]{2,1,0:T(8,128)(2,1)S(1)} %late_square.1.refs_8_), channel_id=1, source_target_pairs={{0,1},{1,0},{2,3},{3,2},{4,5},{5,4},{6,7},{7,6},{8,9},{9,8},{10,11... | collective-permute-start | bytes 196616 | tf_op jit(solution)/shard_map/ppermute | solution.py:21
  24.2 1.3 %collective-permute-start.11 = (bf16[2,128,128]{2,1,0:T(8,128)(2,1)S(1)}, bf16[2,128,128]{2,1,0:T(8,128)(2,1)S(1)}, u32[]{:S(2)}, u32[]{:S(2)}) collective-permute-start(bf16[2,128,128]{2,1,0:T(8,128)(2,1)S(1)} %collective-permute-done.10.refs_3_), channel_id=1, source_target_pairs={{0,1},{1,0},{2,3},{3,2},{4,5},{5,4},{6,7},{7,6},{8,9},{9,8},{10,11... | collective-permute-start | bytes 196616 | tf_op jit(solution)/shard_map/ppermute | solution.py:21
